TPU v7x, 32 devices: a whole 2x2x4 slice. The times are simulated.
32 devices in a mesh: ckpt: 2 (over y), key: 4 (over x, core), qry: 4 (over z).
Axes of the slice: x: 2, y: 2, z: 4, core: 2. Of those that a mesh axis runs over, the one named last changes fastest.
Arguments:
- queries: bfloat16 [1024, 4096], P(('ckpt', 'qry'), 'key'), parts along dimension 0, may hold values from -8 to 8
- keys: bfloat16 [8192, 1024], P(('ckpt', 'key')), parts along dimension 0, may hold values from -8 to 8
- values: bfloat16 [8192, 1024], P(('ckpt', 'key')), parts along dimension 0, may hold values from -6 to 6
- out_grad: bfloat16 [1024, 4096], P(('ckpt', 'qry'), 'key'), parts along dimension 0, may hold values from -6 to 6
Outputs:
- attn_out: bfloat16 [1024, 4096], P(('ckpt', 'qry'), 'key'), parts along dimension 0
- query_out: bfloat16 [1024, 4096], P(('ckpt', 'qry'), 'key'), parts along dimension 0
- key_out: bfloat16 [8192, 1024], P(('ckpt', 'key'), 'qry'), parts along dimension 0
- value_out: bfloat16 [8192, 1024], P(('ckpt', 'key'), 'qry'), parts along dimension 0
There are 2 independent parts, one for each index of `ckpt`. A program takes and returns all parts, laid end to end along the dimension named above; each array names one. Nothing has to cross between parts.
All inputs are finite; a program needn't handle non-finite values.
Results may differ from a plain program's by a relative error of at most 0.03.
Values may be sent and summed in bfloat16 or wider, within the bound.
No kernel may reach another device: no remote copies, remote signals or barrier semaphores. Data moves between devices by JAX's collectives and lax.ppermute only.
A program may use at most 64 MiB of HBM per device.

v0:
```python
import math

import jax
import jax.numpy as jnp
from jax import lax
from jax.sharding import PartitionSpec as P

HQ = 32
KVH = 8
HD = 128


def rounded_values(value):
    return lax.optimization_barrier(value.astype(jnp.bfloat16)).astype(jnp.float32)


def logits_of(query_part, key_part, factor):
    return (
        jnp.einsum("grd,kd->grk", query_part, key_part, preferred_element_type=jnp.float32) * factor
    )


def backward_core(query_part, grad_part, log_norm, row_delta, key_part, value_portion, factor):
    probs = jnp.exp(logits_of(query_part, key_part, factor) - log_norm[..., None])
    grad_prob = jnp.einsum(
        "grd,kd->grk", grad_part, value_portion, preferred_element_type=jnp.float32
    )
    grad_logit = (probs * (grad_prob - row_delta[..., None])).astype(jnp.bfloat16)
    return (probs, grad_logit)


def kv_from(probs, grad_logit, query_part, grad_part, factor):
    value_grad = jnp.einsum(
        "grk,grd->kd", probs.astype(jnp.bfloat16), grad_part, preferred_element_type=jnp.float32
    )
    key_grad = (
        jnp.einsum("grk,grd->kd", grad_logit, query_part, preferred_element_type=jnp.float32)
        * factor
    )
    return (key_grad, value_grad)


def kv_grads(query_part, grad_part, log_norm, row_delta, key_part, value_portion, factor):
    probs, grad_logit = backward_core(
        query_part, grad_part, log_norm, row_delta, key_part, value_portion, factor
    )
    return kv_from(probs, grad_logit, query_part, grad_part, factor)


def per_device(queries, keys, values, out_grad):
    factor = 1.0 / math.sqrt(HD)
    per_group = HQ // KVH
    query_rows, grad_rows = (
        lax.all_gather(queries, "key", axis=1, tiled=True),
        lax.all_gather(out_grad, "key", axis=1, tiled=True),
    )
    row_count = query_rows.shape[0]
    key_count = keys.shape[0]
    query_heads = query_rows.reshape(row_count, KVH, per_group, HD).transpose(1, 2, 0, 3)
    grad_heads = grad_rows.reshape(row_count, KVH, per_group, HD).transpose(1, 2, 0, 3)
    key_heads = keys.reshape(key_count, KVH, HD).transpose(1, 0, 2)
    value_heads = values.reshape(key_count, KVH, HD).transpose(1, 0, 2)

    def block_forward_pass(inputs):
        query_part, key_part, value_portion = inputs
        logits = logits_of(query_part, key_part, factor)
        local_peak = jnp.max(logits, axis=-1)
        exponent_terms = jnp.exp(logits - local_peak[..., None])
        summed = jnp.einsum(
            "grk,kd->grd",
            exponent_terms.astype(jnp.bfloat16),
            value_portion,
            preferred_element_type=jnp.float32,
        )
        return (local_peak, jnp.sum(exponent_terms, axis=-1), summed)

    local_peak, local_sum, summed = lax.map(
        block_forward_pass, (query_heads, key_heads, value_heads)
    )
    peak = lax.pmax(local_peak, "key")
    weight = jnp.exp(local_peak - peak)
    totals = lax.psum(local_sum * weight, "key")
    log_norm = peak + jnp.log(totals)
    scaled = summed * (weight / totals)[..., None]
    partial_value = scaled.transpose(2, 0, 1, 3).reshape(row_count, HQ * HD)
    attn_out = lax.psum_scatter(
        partial_value.astype(jnp.bfloat16), "key", scatter_dimension=1, tiled=True
    )
    products = out_grad.astype(jnp.float32) * attn_out.astype(jnp.float32)
    own_delta = jnp.sum(products.reshape(row_count, -1, HD), axis=-1)
    row_delta = lax.all_gather(own_delta, "key", axis=1, tiled=True)
    delta_heads = row_delta.T.reshape(KVH, per_group, row_count)
    backward_inputs = (query_heads, grad_heads, log_norm, delta_heads, key_heads, value_heads)

    def query_only(inputs):
        probs, grad_logit = backward_core(*inputs, factor)
        return (
            jnp.einsum("grk,kd->grd", grad_logit, inputs[4], preferred_element_type=jnp.float32)
            * factor
        )

    query_grad = lax.map(query_only, backward_inputs)
    n_qry = lax.axis_size("qry")
    kv_local = KVH // n_qry
    query_mine, grad_mine = (
        lax.all_to_all(query_rows, "qry", split_axis=1, concat_axis=0, tiled=True),
        lax.all_to_all(grad_rows, "qry", split_axis=1, concat_axis=0, tiled=True),
    )
    norm_mine, delta_mine = (
        lax.all_to_all(
            log_norm.reshape(HQ, row_count), "qry", split_axis=0, concat_axis=1, tiled=True
        ),
        lax.all_to_all(
            delta_heads.reshape(HQ, row_count), "qry", split_axis=0, concat_axis=1, tiled=True
        ),
    )
    start = lax.axis_index("qry") * kv_local
    key_mine = lax.dynamic_slice_in_dim(key_heads, start, kv_local, 0)
    value_mine = lax.dynamic_slice_in_dim(value_heads, start, kv_local, 0)

    def split_rows(stacked):
        return stacked.reshape(n_qry, row_count, kv_local, per_group, HD).transpose(0, 2, 3, 1, 4)

    def split_stats(stacked):
        return stacked.reshape(kv_local, per_group, n_qry, row_count).transpose(2, 0, 1, 3)

    def per_block(running, pieces):
        key_grad, value_grad = jax.vmap(kv_grads, in_axes=(0, 0, 0, 0, 0, 0, None))(
            pieces[0], pieces[1], pieces[2], pieces[3], key_mine, value_mine, factor
        )
        return (
            (running[0] + rounded_values(key_grad), running[1] + rounded_values(value_grad)),
            None,
        )

    empty = jnp.zeros((kv_local, key_count, HD), jnp.float32)
    sums, unused = lax.scan(
        per_block,
        (empty, empty),
        (
            split_rows(query_mine),
            split_rows(grad_mine),
            split_stats(norm_mine),
            split_stats(delta_mine),
        ),
    )
    key_out = sums[0].transpose(1, 0, 2).reshape(key_count, kv_local * HD)
    value_out = sums[1].transpose(1, 0, 2).reshape(key_count, kv_local * HD)
    query_flat = query_grad.transpose(2, 0, 1, 3).reshape(row_count, HQ * HD)
    query_out = lax.psum_scatter(
        query_flat.astype(jnp.bfloat16), "key", scatter_dimension=1, tiled=True
    )
    return (attn_out, query_out, key_out.astype(jnp.bfloat16), value_out.astype(jnp.bfloat16))


def solution(mesh):
    in_specs = (
        P(("ckpt", "qry"), "key"),
        P(("ckpt", "key"), None),
        P(("ckpt", "key"), None),
        P(("ckpt", "qry"), "key"),
    )
    out_specs = (
        P(("ckpt", "qry"), "key"),
        P(("ckpt", "qry"), "key"),
        P(("ckpt", "key"), "qry"),
        P(("ckpt", "key"), "qry"),
    )
    return jax.shard_map(
        per_device, mesh=mesh, in_specs=in_specs, out_specs=out_specs, check_vma=False
    )
```

profile of v0, /device:TPU:0, one launch (start us, length us, event | category | flops | bytes accessed | tf_op | source)
XLA Modules:
  0.0 259.3 jit_solution(14281453036364921101)
XLA Ops:
  10.9 2.9 %copy.84 = bf16[1024,1024]{0,1:T(8,128)(2,1)S(1)} copy(bf16[1024,1024]{1,0:T(8,128)(2,1)} %param.11) | data formatting | bytes 4194304 | tf_op args[1]
  13.8 2.4 copy.87
  16.2 3.9 %copy.85 = bf16[1024,1024]{0,1:T(8,128)(2,1)} copy(bf16[1024,1024]{1,0:T(8,128)(2,1)} %param.12) | data formatting | bytes 4194304 | tf_op args[2]
  20.1 3.9 %copy.88 = bf16[8,1024,128]{2,1,0:T(8,128)(2,1)} copy(bf16[8,1024,128]{1,2,0:T(8,128)(2,1)} %bitcast.233) | data formatting | bytes 4194304 | tf_op jit(solution)/shard_map/while | solution.py:77
  24.0 5.5 %all-gather.3.cloned.1.call-done = bf16[128,4096]{0,1:T(8,128)(2,1)} async-done(((bf16[128,1024]{0,1:T(8,128)(2,1)}), bf16[128,4096]{0,1:T(8,128)(2,1)}) %all-gather.3.cloned.1.call-update) | async-done | bytes 1048592 | tf_op jit(solution)/shard_map/all_gather | solution.py:54
  31.2 33.5 %while.40 = (s32[]{:T(128)}, f32[8,4,128]{2,1,0:T(4,128)S(1)}, f32[8,4,128]{2,1,0:T(4,128)S(1)}, f32[8,4,128,128]{3,2,1,0:T(8,128)}, bf16[8,4,128,128]{3,2,1,0:T...) while((s32[]{:T(128)}, f32[8,4,128]{2,1,0:T(4,128)S(1)}, ...), condition=%wide.region_3.4_spmd.clone, body=%wide.region_0.3_spmd.sunk.clone | while | flops 272628736 | bytes 7227481 | solution.py:77
  33.2 2.2 fusion.125
  37.4 2.2 fusion.125
  41.6 2.2 fusion.125
  45.7 2.2 fusion.125
  49.9 2.2 fusion.125
  54.1 2.2 fusion.125
  58.3 2.2 fusion.125
  62.5 2.2 fusion.125
  64.7 10.2 %pmax.7 = f32[8,4,128]{2,1,0:T(4,128)S(1)} all-reduce(f32[8,4,128]{2,1,0:T(4,128)S(1)} %get-tuple-element.134), channel_id=1, replica_groups=mesh['ckpt'=2,'key'=4,'qry'=4] {'key'}, use_global_device_ids=true, to_apply=%region_4.5 | all-reduce | flops 4096 | bytes 32768 | tf_op jit(solution)/shard_map/pmax | solution.py:80
  74.9 10.1 %psum.7 = f32[8,4,128]{2,1,0:T(4,128)S(1)} all-reduce(f32[8,4,128]{2,1,0:T(4,128)S(1)} %bitcast.251), channel_id=1, replica_groups=mesh['ckpt'=2,'key'=4,'qry'=4] {'key'}, use_global_device_ids=true, to_apply=%region_5.6 | all-reduce | flops 4096 | bytes 32768 | tf_op jit(solution)/shard_map/psum | solution.py:82
  85.0 10.2 %all_to_all.64 = f32[4,8,128]{2,1,0:T(8,128)S(1)} all-to-all(f32[4,8,128]{2,1,0:T(8,128)S(1)} %get-tuple-element.349), channel_id=1, replica_groups=mesh['ckpt'=2,'key'=4,'qry'=4] {'qry'}, dimensions={0} | all-to-all | bytes 32768 | tf_op jit(solution)/shard_map/all_to_all | solution.py:110
  95.2 3.5 %all-to-all-start = ((bf16[128,4,1024]{0,2,1:T(8,128)(2,1)}), bf16[128,4,1024]{0,2,1:T(8,128)(2,1)S(1)}, u32[]{:S(2)}, u32[]{:S(2)}) async-start(bf16[128,4,1024]{0,2,1:T(8,128)(2,1)} %bitcast.237), calls=%async_computation.2 | async-start | bytes 2097152 | tf_op jit(solution)/shard_map/all_to_all | solution.py:106
  102.5 2.6 %convert_element_type.68 = bf16[128,4096]{1,0:T(8,128)(2,1)} reshape(bf16[128,8,4,128]{3,2,1,0:T(4,128)(2,1)} %copy.89) | data formatting | bytes 2097152 | tf_op jit(solution)/shard_map/convert_element_type | solution.py:87
  105.2 17.7 %all-to-all-done = bf16[128,4,1024]{0,2,1:T(8,128)(2,1)S(1)} async-done(((bf16[128,4,1024]{0,2,1:T(8,128)(2,1)}), bf16[128,4,1024]{0,2,1:T(8,128)(2,1)S(1)}, u32[]{:S(2)}, u32[]{:S(2)}) %all-to-all-start) | async-done | bytes 1048608 | tf_op jit(solution)/shard_map/all_to_all | solution.py:106
  122.9 4.2 %all-to-all-start.2 = ((bf16[128,4,1024]{0,2,1:T(8,128)(2,1)}), bf16[128,4,1024]{0,2,1:T(8,128)(2,1)}, u32[]{:S(2)}, u32[]{:S(2)}) async-start(bf16[128,4,1024]{0,2,1:T(8,128)(2,1)} %bitcast.240), calls=%async_computation.4 | async-start | bytes 2097152 | tf_op jit(solution)/shard_map/all_to_all | solution.py:107
  127.2 2.1 dynamic-slice_bitcast_fusion.4
  129.3 2.1 copy.98
  131.4 2.0 copy.100
  136.0 5.6 %all_gather.11 = f32[128,32]{0,1:T(8,128)} all-gather(f32[128,8]{0,1:T(8,128)S(1)} %copy.91), channel_id=1, replica_groups=mesh['ckpt'=2,'key'=4,'qry'=4] {'key'}, dimensions={1}, use_global_device_ids=true | all-gather | bytes 20480 | tf_op jit(solution)/shard_map/all_gather | solution.py:91
  141.6 10.8 %all-to-all-done.2 = bf16[128,4,1024]{0,2,1:T(8,128)(2,1)} async-done(((bf16[128,4,1024]{0,2,1:T(8,128)(2,1)}), bf16[128,4,1024]{0,2,1:T(8,128)(2,1)}, u32[]{:S(2)}, u32[]{:S(2)}) %all-to-all-start.2) | async-done | bytes 1048608 | tf_op jit(solution)/shard_map/all_to_all | solution.py:107
  152.5 3.2 %all-to-all-start.3 = ((f32[4,8,128]{2,1,0:T(8,128)}), f32[4,8,128]{2,1,0:T(8,128)S(1)}, u32[]{:S(2)}, u32[]{:S(2)}) async-start(f32[4,8,128]{2,1,0:T(8,128)} %bitcast.46), calls=%async_computation.5 | async-start | bytes 32768 | tf_op jit(solution)/shard_map/all_to_all | solution.py:113
  156.0 37.7 %while.41 = (s32[]{:T(128)}, bf16[8,4,128,128]{3,2,1,0:T(8,128)(2,1)}, bf16[8,4,128,128]{3,2,1,0:T(8,128)(2,1)}, bf16[8,1024,128]{2,1,0:T(8,128)(2,1)}, f32[8,4,...) while((s32[]{:T(128)}, ...), condition=%wide.region_9.10_spmd.clone, body=%wide.region_8.9_spmd.sunk.clone | while | flops 405340160 | bytes 5520481 | solution.py:102
  158.1 2.6 fusion.132
  162.9 2.6 fusion.132
  167.6 2.6 fusion.132
  172.3 2.6 fusion.132
  177.0 2.6 fusion.132
  181.7 2.6 fusion.132
  186.4 2.6 fusion.132
  191.1 2.6 fusion.132
  193.7 3.0 %copy.96 = bf16[128,8,4,128]{3,2,1,0:T(4,128)(2,1)} copy(bf16[128,8,4,128]{3,0,2,1:T(8,128)(2,1)} %bitcast.238) | data formatting | bytes 2097152 | tf_op jit(solution)/shard_map/convert_element_type | solution.py:151
  196.7 2.7 %convert_element_type.73 = bf16[128,4096]{1,0:T(8,128)(2,1)} reshape(bf16[128,8,4,128]{3,2,1,0:T(4,128)(2,1)} %copy.96) | data formatting | bytes 2097152 | tf_op jit(solution)/shard_map/convert_element_type | solution.py:151
  199.5 51.5 %while.42 = (s32[]{:T(128)}, f32[2,1024,128]{2,1,0:T(8,128)S(1)}, f32[2,1024,128]{2,1,0:T(8,128)S(1)}, bf16[4,2,4,128,128]{3,4,2,1,0:T(8,128)(2,1)}, bf16[2,1024...) while((s32[]{:T(128)}, f32[2,1024,128]{2,1,0:T(8,128)S(1)}, ...), condition=%wide.region_12.13_spmd.clone.clone, body=%wide.region_11.12_spmd.clone.sunk.clone | while | flops 1084489728 | bytes 37778584 | solution.py:137
  201.3 2.0 copy-done
  203.3 2.3 fusion.141
  205.5 5.5 %fusion.142 = bf16[2,1024,128]{2,1,0:T(8,128)(2,1)} fusion(f32[2,4,128,1024]{3,2,1,0:T(8,128)} %copy-done, f32[2,4,128]{2,1,0:T(4,128)S(1)} %dynamic-slice_bitcast_fusion.14, f32[2,4,128]{2,1,0:T(4,128)S(1)} %dynamic-slice_bitcast_fusion.13, bf16[2,1024,128]{2,1,0:T(8,128)(2,1)} %get-tuple-element.623, ...), kind=kOutput, calls=%fused_computation.54.clone.1.clone | convolution fusion | flops 542638080 | bytes 5776384 | tf_op jit(solution)/shard_map/while/body/eval_jaxpr/vmap(grk,grd->kd)/dot_general | solution.py:37
  216.3 2.3 fusion.141
  218.6 5.2 %fusion.142 = bf16[2,1024,128]{2,1,0:T(8,128)(2,1)} fusion(f32[2,4,128,1024]{3,2,1,0:T(8,128)} %copy-done, f32[2,4,128]{2,1,0:T(4,128)S(1)} %dynamic-slice_bitcast_fusion.14, f32[2,4,128]{2,1,0:T(4,128)S(1)} %dynamic-slice_bitcast_fusion.13, bf16[2,1024,128]{2,1,0:T(8,128)(2,1)} %get-tuple-element.623, ...), kind=kOutput, calls=%fused_computation.54.clone.1.clone | convolution fusion | flops 542638080 | bytes 5776384 | tf_op jit(solution)/shard_map/while/body/eval_jaxpr/vmap(grk,grd->kd)/dot_general | solution.py:37
  229.2 2.3 fusion.141
  231.5 5.2 %fusion.142 = bf16[2,1024,128]{2,1,0:T(8,128)(2,1)} fusion(f32[2,4,128,1024]{3,2,1,0:T(8,128)} %copy-done, f32[2,4,128]{2,1,0:T(4,128)S(1)} %dynamic-slice_bitcast_fusion.14, f32[2,4,128]{2,1,0:T(4,128)S(1)} %dynamic-slice_bitcast_fusion.13, bf16[2,1024,128]{2,1,0:T(8,128)(2,1)} %get-tuple-element.623, ...), kind=kOutput, calls=%fused_computation.54.clone.1.clone | convolution fusion | flops 542638080 | bytes 5776384 | tf_op jit(solution)/shard_map/while/body/eval_jaxpr/vmap(grk,grd->kd)/dot_general | solution.py:37
  242.0 2.3 fusion.141
  244.3 5.2 %fusion.142 = bf16[2,1024,128]{2,1,0:T(8,128)(2,1)} fusion(f32[2,4,128,1024]{3,2,1,0:T(8,128)} %copy-done, f32[2,4,128]{2,1,0:T(4,128)S(1)} %dynamic-slice_bitcast_fusion.14, f32[2,4,128]{2,1,0:T(4,128)S(1)} %dynamic-slice_bitcast_fusion.13, bf16[2,1024,128]{2,1,0:T(8,128)(2,1)} %get-tuple-element.623, ...), kind=kOutput, calls=%fused_computation.54.clone.1.clone | convolution fusion | flops 542638080 | bytes 5776384 | tf_op jit(solution)/shard_map/while/body/eval_jaxpr/vmap(grk,grd->kd)/dot_general | solution.py:37
  (104 shorter events, 65.8 us)
Async XLA Ops:
  7.2 22.4 %all-gather.3.cloned.1.call-start = ((), (), s32[]{:S(2)}) async-start(), calls=%async_computation.6 | async-start | bytes 1310720 | tf_op jit(solution)/shard_map/all_gather | solution.py:54
  9.0 96.1 %all-gather.5.cloned.1.call-start = ((), (), s32[]{:S(2)}) async-start(), calls=%async_computation.8 | async-start | bytes 1310720 | tf_op jit(solution)/shard_map/all_gather | solution.py:55
  64.7 30.5 %copy-start.4 = (bf16[8,4,128,128]{3,2,1,0:T(8,128)(2,1)}, bf16[8,4,128,128]{3,2,1,0:T(8,128)(2,1)S(1)}, u32[]{:S(2)}) copy-start(bf16[8,4,128,128]{3,2,1,0:T(8,128)(2,1)S(1)} %get-tuple-element.632) | copy-start | bytes 3145732
  95.2 27.7 %all-to-all-start = ((bf16[128,4,1024]{0,2,1:T(8,128)(2,1)}), bf16[128,4,1024]{0,2,1:T(8,128)(2,1)S(1)}, u32[]{:S(2)}, u32[]{:S(2)}) async-start(bf16[128,4,1024]{0,2,1:T(8,128)(2,1)} %bitcast.237), calls=%async_computation.2 | async-start | bytes 2097152 | tf_op jit(solution)/shard_map/all_to_all | solution.py:106
  98.7 35.9 %reduce-scatter.3.cloned.1.call-start = ((), (), s32[]{:S(2)}) async-start(), calls=%async_computation.7 | async-start | bytes 1310720 | tf_op jit(solution)/shard_map/reduce_scatter | solution.py:86
  122.9 4.3 %copy-start.3 = (bf16[128,4,1024]{0,2,1:T(8,128)(2,1)}, bf16[128,4,1024]{0,2,1:T(8,128)(2,1)S(1)}, u32[]{:S(2)}) copy-start(bf16[128,4,1024]{0,2,1:T(8,128)(2,1)S(1)} %all-to-all-done) | copy-start | bytes 3145732
  122.9 29.6 %all-to-all-start.2 = ((bf16[128,4,1024]{0,2,1:T(8,128)(2,1)}), bf16[128,4,1024]{0,2,1:T(8,128)(2,1)}, u32[]{:S(2)}, u32[]{:S(2)}) async-start(bf16[128,4,1024]{0,2,1:T(8,128)(2,1)} %bitcast.240), calls=%async_computation.4 | async-start | bytes 2097152 | tf_op jit(solution)/shard_map/all_to_all | solution.py:107
  129.3 5.3 %copy-start.5 = (bf16[128,1024]{1,0:T(8,128)(2,1)S(1)}, bf16[128,1024]{1,0:T(8,128)(2,1)}, u32[]{:S(2)}) copy-start(bf16[128,1024]{1,0:T(8,128)(2,1)} %param.13) | copy-start | bytes 786436
  152.5 47.0 %all-to-all-start.3 = ((f32[4,8,128]{2,1,0:T(8,128)}), f32[4,8,128]{2,1,0:T(8,128)S(1)}, u32[]{:S(2)}, u32[]{:S(2)}) async-start(f32[4,8,128]{2,1,0:T(8,128)} %bitcast.46), calls=%async_computation.5 | async-start | bytes 32768 | tf_op jit(solution)/shard_map/all_to_all | solution.py:113
  155.7 97.0 %reduce-scatter.5.cloned.1.call-start = ((), (), s32[]{:S(2)}) async-start(), calls=%async_computation.9 | async-start | bytes 1310720 | tf_op jit(solution)/shard_map/reduce_scatter | solution.py:150
  196.7 2.8 %copy-start.1 = (f32[2,1024,128]{2,1,0:T(8,128)S(1)}, f32[2,1024,128]{2,1,0:T(8,128)}, u32[]{:S(2)}) copy-start(f32[2,1024,128]{2,1,0:T(8,128)} %custom-call.1) | copy-start | bytes 3145732
  196.7 2.8 %copy-start.2 = (bf16[2,1024,128]{2,1,0:T(8,128)(2,1)S(1)}, bf16[2,1024,128]{2,1,0:T(8,128)(2,1)}, u32[]{:S(2)}) copy-start(bf16[2,1024,128]{2,1,0:T(8,128)(2,1)} %copy.98) | copy-start | bytes 1572868
  201.2 2.0 copy-start
  214.3 2.0 copy-start
  227.2 2.0 copy-start
  240.0 2.0 copy-start
Sparse Core Ops, SparseCore 0:
  10.1 19.4 all-gather.2
  31.7 16.7 all-gather.4
  105.3 26.2 reduce-scatter.2
  199.6 25.0 reduce-scatter.4
where the time goes:
time: 262 us; the launch traced here: 259 us
  matrix products  98.5 us (38%)
  local copies, waits for them, and re-layouts  48.4 us (18%)
  blocking collectives  36.1 us (14%)
  waiting for transfers between devices  34.2 us (13%)
  other arithmetic  16.5 us (6%)
  between operations  13.9 us (5%)
  starting transfers between devices  11.4 us (4%)
    dot_general x20, matrix products, logits_of(): jnp.einsum('grd,kd->grk', query_part, key_part, preferred_element_type=jn...  30.2 us
    dot_general x4, matrix products, kv_from(): jnp.einsum('grk,grd->kd', grad_logit, query_part, preferred_element_type=...  21.1 us
    dot_general x8, matrix products, query_only(): jnp.einsum('grk,kd->grd', grad_logit, inputs[4], preferred_element_type=j...  20.7 us
    all_to_all x1, waiting for transfers between devices, per_device(): lax.all_to_all(query_rows, 'qry', split_axis=1, concat_axis=0, tiled=True)  17.7 us
    dot_general x8, matrix products, block_forward_pass(): jnp.einsum('grk,kd->grd', exponent_terms.astype(jnp.bfloat16), value_port...  17.5 us
    unnamed x17, local copies, waits for them, and re-layouts  14.6 us
    all_to_all x1, waiting for transfers between devices, per_device(): lax.all_to_all(grad_rows, 'qry', split_axis=1, concat_axis=0, tiled=True)  10.8 us
    pmax x1, blocking collectives, per_device(): peak = lax.pmax(local_peak, 'key')  10.2 us
  transfers between devices with their start and end apart: 7, of which 3 were waited for; matrix products, arithmetic and copies ran while one was open for 59% of the time, Pallas kernels for 0%

commit v1 on v0

v1 whole, which is shorter than its diff:
```python
import functools
import math

import jax
import jax.numpy as jnp
from jax import lax
from jax.experimental import pallas as pl
from jax.experimental.pallas import tpu as pltpu
from jax.sharding import PartitionSpec as P

HQ = 32
KVH = 8
HD = 128
GROUP = HQ // KVH
FACTOR = 1.0 / math.sqrt(HD)
SCALE2 = FACTOR * math.log2(math.e)

NT = (((1,), (1,)), ((), ()))
NN = (((1,), (0,)), ((), ()))


def dot(a, b, dims):
    return lax.dot_general(a, b, dims, preferred_element_type=jnp.float32)


def head(block, h):
    return block[:, h * HD : (h + 1) * HD]


def stack_heads(block, heads):
    return jnp.concatenate([head(block, h) for h in heads], axis=0)


def columns_of(rows):
    n, width = rows.shape
    pad = jnp.zeros((128 - n, width), jnp.float32)
    return jnp.concatenate([rows, pad], axis=0).T


def fwd_kernel(hp, chain, scal, q_ref, g_ref, k_ref, v_ref, o_ref, st_ref):
    rows = q_ref.shape[0]
    q, g = q_ref[...], g_ref[...]
    k, v = k_ref[...], v_ref[...]
    lane = lax.broadcasted_iota(jnp.int32, (rows, 128), 1)
    tile = jnp.zeros((rows, 128), jnp.float32)
    for first in range(0, hp, chain):
        heads = range(first, min(hp, first + chain))
        s = dot(stack_heads(q, heads), k, NT)
        m = jnp.max(s, axis=1, keepdims=True)
        p = jnp.exp2((s - m) * SCALE2)
        l = jnp.sum(p, axis=1, keepdims=True)
        o = dot(p.astype(jnp.bfloat16), v, NN)
        d = jnp.sum(o * stack_heads(g, heads).astype(jnp.float32), axis=1, keepdims=True)
        for n, h in enumerate(heads):
            part = slice(n * rows, (n + 1) * rows)
            o_ref[:, h * HD : (h + 1) * HD] = o[part].astype(jnp.bfloat16)
            tile = jnp.where(lane == h, m[part], tile)
            tile = jnp.where(lane == hp + h, l[part], tile)
            tile = jnp.where(lane == 2 * hp + h, d[part], tile)
    st_ref[0] = tile.T[: 4 * hp]


def fwd_call(qg, keys, values, scal, hp):
    rows = qg.shape[0]
    hps = qg.shape[1] // (2 * HD)
    ups = hps // hp
    nk = keys.shape[0]

    def kv_map(i, s):
        return (0, ((s[0] * ups + i) * hp) // GROUP)

    return pl.pallas_call(
        functools.partial(fwd_kernel, hp, 2),
        grid_spec=pltpu.PrefetchScalarGridSpec(
            num_scalar_prefetch=1,
            grid=(ups,),
            in_specs=[
                pl.BlockSpec((rows, hp * HD), lambda i, s: (0, i)),
                pl.BlockSpec((rows, hp * HD), lambda i, s: (0, ups + i)),
                pl.BlockSpec((nk, HD), kv_map),
                pl.BlockSpec((nk, HD), kv_map),
            ],
            out_specs=[
                pl.BlockSpec((rows, hp * HD), lambda i, s: (0, i)),
                pl.BlockSpec((1, 4 * hp, rows), lambda i, s: (i, 0, 0)),
            ],
        ),
        out_shape=[
            jax.ShapeDtypeStruct((rows, hps * HD), jnp.bfloat16),
            jax.ShapeDtypeStruct((ups, 4 * hp, rows), jnp.float32),
        ],
        cost_estimate=pl.CostEstimate(
            flops=8 * rows * hps * nk * HD, bytes_accessed=2 << 20, transcendentals=rows * hps * nk
        ),
        name="fwd",
    )(scal, qg, qg, keys, values)


def stats_kernel(hp, ups, st_ref, ld_ref):
    n_key = st_ref.shape[0]
    for u in range(n_key * ups):
        s, i = u // ups, u % ups
        parts = [st_ref[c, (s ^ c) * ups + i] for c in range(n_key)]
        peak = parts[0][:hp]
        for x in parts[1:]:
            peak = jnp.maximum(peak, x[:hp])
        total = jnp.zeros_like(peak)
        delta = jnp.zeros_like(peak)
        for x in parts:
            w = jnp.exp2((x[:hp] - peak) * SCALE2)
            total += w * x[hp : 2 * hp]
            delta += w * x[2 * hp : 3 * hp]
        ld_ref[u] = jnp.concatenate([peak * SCALE2 + jnp.log2(total), delta / total], axis=0)


def stats_call(gathered, hp, ups):
    n_key = gathered.shape[0]
    rows = gathered.shape[-1]
    return pl.pallas_call(
        functools.partial(stats_kernel, hp, ups),
        out_shape=jax.ShapeDtypeStruct((n_key * ups, 2 * hp, rows), jnp.float32),
        cost_estimate=pl.CostEstimate(flops=1 << 20, bytes_accessed=1 << 19, transcendentals=1 << 15),
        name="stats",
    )(gathered)


def out_kernel(hp, ups, n_key, scal, *refs):
    st_ref, ld_ref = refs[0], refs[1]
    parts, out_ref = refs[2 : 2 + n_key], refs[2 + n_key]
    for i in range(ups):
        norm = ld_ref[scal[0] * ups + i][:hp]
        weights = [
            jnp.exp2(st_ref[scal[p + 1], p * ups + i][:hp] * SCALE2 - norm) for p in range(n_key)
        ]
        cols = columns_of(jnp.concatenate(weights, axis=0))
        for h in range(hp):
            at = slice((i * hp + h) * HD, (i * hp + h + 1) * HD)
            total = None
            for p in range(n_key):
                lane = p * hp + h
                term = parts[p][:, at].astype(jnp.float32) * cols[:, lane : lane + 1]
                total = term if total is None else total + term
            out_ref[:, at] = total.astype(jnp.bfloat16)


def out_call(gathered, ld, parts, scal, hp, ups):
    n_key = len(parts)
    vmem = pl.BlockSpec(memory_space=pltpu.VMEM)
    return pl.pallas_call(
        functools.partial(out_kernel, hp, ups, n_key),
        in_specs=[pl.BlockSpec(memory_space=pltpu.SMEM)] + [vmem] * (2 + n_key),
        out_specs=vmem,
        out_shape=jax.ShapeDtypeStruct(parts[0].shape, jnp.bfloat16),
        cost_estimate=pl.CostEstimate(flops=1 << 22, bytes_accessed=2 << 20, transcendentals=1 << 12),
        name="attn_out",
    )(scal, gathered, ld, *parts)


def dq_kernel(hp, chain, scal, q_ref, g_ref, k_ref, v_ref, ld_ref, dq_ref):
    rows = q_ref.shape[0]
    q, g = q_ref[...], g_ref[...]
    k, v = k_ref[...], v_ref[...]
    cols = columns_of(ld_ref[0])
    for first in range(0, hp, chain):
        heads = range(first, min(hp, first + chain))
        norm = jnp.concatenate([cols[:, h : h + 1] for h in heads], axis=0)
        delta = jnp.concatenate([cols[:, hp + h : hp + h + 1] for h in heads], axis=0)
        s = dot(stack_heads(q, heads), k, NT)
        p = jnp.exp2(s * SCALE2 - norm)
        gp = dot(stack_heads(g, heads), v, NT)
        ds = (p * (gp - delta)).astype(jnp.bfloat16)
        dq = dot(ds, k, NN) * FACTOR
        for n, h in enumerate(heads):
            dq_ref[:, h * HD : (h + 1) * HD] = dq[n * rows : (n + 1) * rows].astype(jnp.bfloat16)


def dq_call(qg, keys, values, ld, scal, hp):
    rows = qg.shape[0]
    hps = qg.shape[1] // (2 * HD)
    ups = hps // hp
    nk = keys.shape[0]

    def kv_map(i, s):
        return (0, ((s[0] * ups + i) * hp) // GROUP)

    return pl.pallas_call(
        functools.partial(dq_kernel, hp, 2),
        grid_spec=pltpu.PrefetchScalarGridSpec(
            num_scalar_prefetch=1,
            grid=(ups,),
            in_specs=[
                pl.BlockSpec((rows, hp * HD), lambda i, s: (0, i)),
                pl.BlockSpec((rows, hp * HD), lambda i, s: (0, ups + i)),
                pl.BlockSpec((nk, HD), kv_map),
                pl.BlockSpec((nk, HD), kv_map),
                pl.BlockSpec((1, 2 * hp, rows), lambda i, s: (s[0] * ups + i, 0, 0)),
            ],
            out_specs=pl.BlockSpec((rows, hp * HD), lambda i, s: (0, i)),
        ),
        out_shape=jax.ShapeDtypeStruct((rows, hps * HD), jnp.bfloat16),
        cost_estimate=pl.CostEstimate(
            flops=12 * rows * hps * nk * HD, bytes_accessed=2 << 20, transcendentals=rows * hps * nk
        ),
        name="dq",
    )(scal, qg, qg, keys, values, ld)


def pack_kernel(n_qry, per_z, width, scal, *refs):
    n_key = len(refs) - 3
    parts, out_ref, sem = refs[:n_key], refs[n_key], refs[n_key + 1]
    tmp = refs[n_key + 2]
    hps_w = parts[0].shape[1] // 2
    half = pl.multiple_of(scal[1] * width, 128)

    def copies(z, i, p):
        at = i * width
        first = pltpu.make_async_copy(
            parts[p].at[:, pl.ds(half, width)], tmp.at[z, :, pl.ds(at, width)], sem.at[z, i, 0]
        )
        second = pltpu.make_async_copy(
            parts[p].at[:, pl.ds(hps_w + half, width)],
            tmp.at[z, :, pl.ds(per_z * width + at, width)],
            sem.at[z, i, 1],
        )
        return first, second

    for z in range(n_qry):
        for i in range(per_z):
            where = jnp.bitwise_xor(scal[0], z * per_z + i)
            for p in range(n_key):

                @pl.when(where == p)
                def _():
                    for c in copies(z, i, p):
                        c.start()

    for z in range(n_qry):
        for i in range(per_z):
            for c in copies(z, i, 0):
                c.wait()
        out_ref[z] = tmp[z]


def pack_call(parts, scal, n_qry, per_z, width):
    rows = parts[0].shape[0]
    shape = (n_qry, rows, 2 * per_z * width)
    return pl.pallas_call(
        functools.partial(pack_kernel, n_qry, per_z, width),
        in_specs=[pl.BlockSpec(memory_space=pltpu.SMEM)]
        + [pl.BlockSpec(memory_space=pl.ANY)] * len(parts),
        out_specs=pl.BlockSpec(memory_space=pltpu.VMEM),
        out_shape=jax.ShapeDtypeStruct(shape, jnp.bfloat16),
        scratch_shapes=[
            pltpu.SemaphoreType.DMA((n_qry, per_z, 2)),
            pltpu.VMEM(shape, jnp.bfloat16),
        ],
        cost_estimate=pl.CostEstimate(flops=1 << 20, bytes_accessed=2 << 20, transcendentals=0),
        name="pack",
    )(scal, *parts)


def dkv_kernel(hp, scal, q_ref, g_ref, k_ref, v_ref, ld_ref, *refs):
    dk_ref, dv_ref = refs[-2:]
    n_qry, rows = q_ref.shape[0], q_ref.shape[1]
    sub = GROUP // hp
    k, v = k_ref[...], v_ref[...]
    dk = dv = None
    for z in range(n_qry):
        q, g = q_ref[z], g_ref[z]
        heads = range(GROUP)
        qs, gs = stack_heads(q, heads), stack_heads(g, heads)
        units = [ld_ref[z, u] for u in range(sub)]
        norm = jnp.concatenate([units[h // hp][h % hp : h % hp + 1] for h in heads], axis=1)
        delta = jnp.concatenate(
            [units[h // hp][hp + h % hp : hp + h % hp + 1] for h in heads], axis=1
        )
        s = dot(k, qs, NT)
        p = jnp.exp2(s * SCALE2 - norm)
        gp = dot(v, gs, NT)
        ds = (p * (gp - delta)).astype(jnp.bfloat16)
        dv_z = dot(p.astype(jnp.bfloat16), gs, NN)
        dk_z = dot(ds, qs, NN)
        dv = dv_z if dv is None else dv + dv_z
        dk = dk_z if dk is None else dk + dk_z
    dk_ref[...] = (dk * FACTOR).astype(jnp.bfloat16)
    dv_ref[...] = dv.astype(jnp.bfloat16)


def dkv_call(qgz, keys, values, ldz, scal, hp, kvl, tile, into=None):
    n_qry, rows, width = qgz.shape
    nh = width // (2 * HD * GROUP)
    nk = keys.shape[0]
    sub = GROUP // hp
    wide = GROUP * HD
    out_map = lambda g, t, s: (t, s[1] + g)
    kv_map = lambda g, t, s: (t, s[0] + g)
    in_specs = [
        pl.BlockSpec((n_qry, rows, wide), lambda g, t, s: (0, 0, g)),
        pl.BlockSpec((n_qry, rows, wide), lambda g, t, s: (0, 0, nh + g)),
        pl.BlockSpec((tile, HD), kv_map),
        pl.BlockSpec((tile, HD), kv_map),
        pl.BlockSpec((n_qry, sub, 2 * hp, rows), lambda g, t, s: (0, s[1] + g, 0, 0)),
    ]
    args = [scal, qgz, qgz, keys, values, ldz]
    aliases = {}
    if into is not None:
        in_specs += [pl.BlockSpec(memory_space=pl.ANY)] * 2
        aliases = {len(args): 0, len(args) + 1: 1}
        args += list(into)
    shape = jax.ShapeDtypeStruct((nk, kvl * HD), jnp.bfloat16)
    return pl.pallas_call(
        functools.partial(dkv_kernel, hp),
        grid_spec=pltpu.PrefetchScalarGridSpec(
            num_scalar_prefetch=1,
            grid=(nh, nk // tile),
            in_specs=in_specs,
            out_specs=[pl.BlockSpec((tile, HD), out_map)] * 2,
        ),
        out_shape=[shape, shape],
        input_output_aliases=aliases,
        cost_estimate=pl.CostEstimate(
            flops=8 * n_qry * rows * GROUP * nh * nk * HD,
            bytes_accessed=4 << 20,
            transcendentals=n_qry * rows * GROUP * nh * nk,
        ),
        name="dkv",
    )(*args)


def per_device(queries, keys, values, out_grad):
    n_key, n_qry = lax.axis_size("key"), lax.axis_size("qry")
    me_k, me_z = lax.axis_index("key"), lax.axis_index("qry")
    rows = queries.shape[0]
    hps = HQ // n_key
    hp = min(hps, GROUP)
    ups = hps // hp
    kvl = KVH // n_qry
    per_z = n_key // n_qry
    split = 2 if (kvl % 2 == 0 and per_z == 1) else 1

    def swap(x, p):
        return lax.ppermute(x, "key", [(i, i ^ p) for i in range(n_key)])

    parts = {0: jnp.concatenate([queries, out_grad], axis=1)}
    bit = n_key // 2
    while bit:
        for p in list(parts):
            parts[p ^ bit] = swap(parts[p], bit)
        bit //= 2

    order = [p for p in (0, 1)] + [p for p in range(2, n_key)]
    slice_of = [jnp.bitwise_xor(me_k, p).astype(jnp.int32) for p in range(n_key)]
    o_part, st_part = {}, {}
    for p in order:
        o_part[p], st_part[p] = fwd_call(parts[p], keys, values, slice_of[p][None], hp)

    half = (me_k % split).astype(jnp.int32)
    packed = pack_call(
        [parts[p] for p in range(n_key)],
        jnp.stack([me_k.astype(jnp.int32), half]),
        n_qry,
        per_z,
        hps * HD // split,
    )
    mine_z = lax.all_to_all(packed, "qry", split_axis=0, concat_axis=0, tiled=True)

    o_recv = [o_part[0]] + [swap(o_part[p], p) for p in range(1, n_key)]
    stats = jnp.concatenate([st_part[p] for p in range(n_key)], axis=0)
    gathered = lax.all_gather(stats, "key", axis=0, tiled=False)
    ld = stats_call(gathered, hp, ups)

    ldz = lax.all_to_all(ld, "qry", split_axis=0, concat_axis=0, tiled=True)
    ldz = ldz.reshape(n_qry, kvl * (GROUP // hp), 2 * hp, rows)

    dq_recv = {}
    for p in reversed(order):
        dq = dq_call(parts[p], keys, values, ld, slice_of[p][None], hp)
        dq_recv[p] = swap(dq, p) if p else dq

    attn_out = out_call(gathered, ld, o_recv, jnp.stack([me_k.astype(jnp.int32)] + slice_of), hp, ups)

    tile = min(512, keys.shape[0])
    z32 = me_z.astype(jnp.int32)
    if split == 2:
        nh = kvl // 2
        first = half * nh
        second = (1 - half) * nh
        other_z = swap(mine_z, 1)
        outs = dkv_call(
            mine_z, keys, values, ldz, jnp.stack([z32 * kvl + first, first]), hp, kvl, tile
        )
        outs = dkv_call(
            other_z, keys, values, ldz, jnp.stack([z32 * kvl + second, second]), hp, kvl, tile, outs
        )
    else:
        outs = dkv_call(
            mine_z, keys, values, ldz, jnp.stack([z32 * kvl, jnp.zeros_like(z32)]), hp, kvl, tile
        )

    query_out = sum(dq_recv[p].astype(jnp.float32) for p in range(n_key)).astype(jnp.bfloat16)
    return (attn_out, query_out, outs[0], outs[1])


def solution(mesh):
    in_specs = (
        P(("ckpt", "qry"), "key"),
        P(("ckpt", "key"), None),
        P(("ckpt", "key"), None),
        P(("ckpt", "qry"), "key"),
    )
    out_specs = (
        P(("ckpt", "qry"), "key"),
        P(("ckpt", "qry"), "key"),
        P(("ckpt", "key"), "qry"),
        P(("ckpt", "key"), "qry"),
    )
    return jax.shard_map(
        per_device, mesh=mesh, in_specs=in_specs, out_specs=out_specs, check_vma=False
    )
```

time: 262 us -> 106 us (0.40)
  matrix products: 98.5 us -> 0 us
  Pallas kernels: 0 us -> 55.7 us
  local copies, waits for them, and re-layouts: 48.4 us -> 4.88 us
  blocking collectives: 36.1 us -> 6.21 us
  waiting for transfers between devices: 34.2 us -> 15.4 us
  between operations: 13.9 us -> 0.75 us
  other arithmetic: 16.5 us -> 4.48 us
  starting transfers between devices: 11.4 us -> 17.9 us
    dot_general x44 -> x0, matrix products: 98.5 us -> none  [the longest x20 30.2 us: logits_of(): jnp.einsum('grd,kd->grk', query_part, key_part, preferred_element_type=jn...]
    pallas_call x0 -> x13, Pallas kernels: none -> 55.7 us  [the longest x4 17.1 us: fwd_call(): pl.pallas_call(functools.partial(fwd_kernel, hp, 2), grid_spec=pltpu.Pref...]
    all_to_all x3 -> x2, waiting for transfers between devices: 28.6 us -> 0.2 us  [the longest x1 0.2 us: per_device(): ldz = lax.all_to_all(ld, 'qry', split_axis=0, concat_axis=0, tiled=True)]
    while x11 -> x0, local copies, waits for them, and re-layouts: 15.8 us -> none
    ppermute x0 -> x10, waiting for transfers between devices: none -> 15.2 us  [swap(): return lax.ppermute(x, 'key', [(i, i ^ p) for i in range(n_key)])]
    unnamed x17 -> x31, local copies, waits for them, and re-layouts: 14.6 us -> 3.25 us
    pmax x1 -> x0, blocking collectives: 10.2 us -> none  [per_device(): peak = lax.pmax(local_peak, 'key')]
    all_to_all x1 -> x0, blocking collectives: 10.2 us -> none  [per_device(): lax.all_to_all(log_norm.reshape(HQ, row_count), 'qry', split_axis=0, conc...]
  transfers between devices with their start and end apart: 7 -> 12, of which waited for: 3 -> 4; matrix products, arithmetic and copies ran while one was open for 59% -> 5% of each run, Pallas kernels for 0% -> 43%
where the time goes in v1:
time: 106 us; the launch traced here: 105 us
  Pallas kernels  55.7 us (53%)
  starting transfers between devices  17.9 us (17%)
  waiting for transfers between devices  15.4 us (15%)
  blocking collectives  6.21 us (6%)
  local copies, waits for them, and re-layouts  4.88 us (5%)
  other arithmetic  4.48 us (4%)
    pallas_call x4, Pallas kernels, fwd_call(): pl.pallas_call(functools.partial(fwd_kernel, hp, 2), grid_spec=pltpu.Pref...  17.1 us
    pallas_call x4, Pallas kernels, dq_call(): pl.pallas_call(functools.partial(dq_kernel, hp, 2), grid_spec=pltpu.Prefe...  16.2 us
    ppermute x10, waiting for transfers between devices, swap(): return lax.ppermute(x, 'key', [(i, i ^ p) for i in range(n_key)])  15.2 us
    pallas_call x2, Pallas kernels, dkv_call(): pl.pallas_call(functools.partial(dkv_kernel, hp), grid_spec=pltpu.Prefetc...  15 us
    ppermute x10, starting transfers between devices, swap(): return lax.ppermute(x, 'key', [(i, i ^ p) for i in range(n_key)])  7.67 us
    all_gather x1, blocking collectives, per_device(): gathered = lax.all_gather(stats, 'key', axis=0, tiled=False)  6.21 us
    all_to_all x1, starting transfers between devices, per_device(): lax.all_to_all(packed, 'qry', split_axis=0, concat_axis=0, tiled=True)  5.13 us
    all_to_all x1, starting transfers between devices, per_device(): ldz = lax.all_to_all(ld, 'qry', split_axis=0, concat_axis=0, tiled=True)  5.09 us
  transfers between devices with their start and end apart: 12, of which 4 were waited for; matrix products, arithmetic and copies ran while one was open for 5% of the time, Pallas kernels for 43%

profile of v1, /device:TPU:0, one launch (start us, length us, event | category | flops | bytes accessed | tf_op | source)
XLA Modules:
  0.0 105.3 jit_solution(6368182580438091848)
XLA Ops:
  0.6 1.0 constant_dynamic-update-slice_fusion.1
  1.6 1.0 constant_dynamic-update-slice_fusion.q_ref.g_ref.refs_0_
  2.6 3.0 %collective-permute-start.1 = (bf16[128,2048]{1,0:T(8,128)(2,1)S(1)}, bf16[128,2048]{1,0:T(8,128)(2,1)S(1)}, u32[]{:S(2)}, u32[]{:S(2)}) collective-permute-start(bf16[128,2048]{1,0:T(8,128)(2,1)S(1)} %constant_dynamic-update-slice_fusion.q_ref.g_ref.refs_0_), channel_id=1, source_target_pairs={{0,8},{4,12},{8,0},{12,4},{1,9},{5,13},{9,1},{13,5},{2,10},{6,14},... | collective-permute-start | bytes 1572872 | tf_op jit(solution)/shard_map/ppermute | solution.py:342
  5.6 0.0 collective-permute-start
  5.6 11.9 %collective-permute-done.1.q_ref.g_ref.refs_2_ = bf16[128,2048]{1,0:T(8,128)(2,1)S(1)} collective-permute-done((bf16[128,2048]{1,0:T(8,128)(2,1)S(1)}, bf16[128,2048]{1,0:T(8,128)(2,1)S(1)}, u32[]{:S(2)}, u32[]{:S(2)}) %collective-permute-start.1) | collective-permute-done | bytes 524320 | tf_op jit(solution)/shard_map/ppermute | solution.py:342
  17.5 0.0 collective-permute-start.2
  17.5 0.7 pad_add_fusion.1.scal
  18.2 0.0 collective-permute-done.q_ref.g_ref.refs_1_
  18.2 1.2 %collective-permute-done.2.q_ref.g_ref.refs_3_ = bf16[128,2048]{1,0:T(8,128)(2,1)S(1)} collective-permute-done((bf16[128,2048]{1,0:T(8,128)(2,1)S(1)}, bf16[128,2048]{1,0:T(8,128)(2,1)S(1)}, u32[]{:S(2)}, u32[]{:S(2)}) %collective-permute-start.2) | collective-permute-done | bytes 524320 | tf_op jit(solution)/shard_map/ppermute | solution.py:342
  19.5 0.0 copy-start.3
  19.5 0.8 copy-done.3
  20.3 3.0 %pack.1 = bf16[4,128,1024]{2,1,0:T(8,128)(2,1)} custom-call(s32[2]{0:T(128)} %pad_add_fusion.1.scal, bf16[128,2048]{1,0:T(8,128)(2,1)} %copy-done, bf16[128,2048]{1,0:T(8,128)(2,1)} %copy-done.1, bf16[128,2048]{1,0:T(8,128)(2,1)} %copy-done.2, bf16[128,2048]{1,0:T(8,128)(2,1)} %copy-done.3), custom_call_target="tpu_custom_call" | custom-call | flops 1048576 | bytes 2097152 | tf_op jit(solution)/shard_map/pack/pallas_call | solution.py:247
  23.3 5.1 %all-to-all-start = ((bf16[4,128,1024]{2,1,0:T(8,128)(2,1)}), bf16[4,128,1024]{2,1,0:T(8,128)(2,1)S(1)}, u32[]{:S(2)}, u32[]{:S(2)}) async-start(bf16[4,128,1024]{2,1,0:T(8,128)(2,1)} %pack.1), calls=%async_computation | async-start | bytes 2097152 | tf_op jit(solution)/shard_map/all_to_all | solution.py:365
  28.4 0.7 stack.43.scal
  29.1 4.3 %fwd.4 = (bf16[128,1024]{1,0:T(8,128)(2,1)}, f32[2,16,128]{2,1,0:T(8,128)}) custom-call(s32[1]{0:T(128)} %bitcast.scal, bf16[128,2048]{1,0:T(8,128)(2,1)} %copy-done, bf16[128,2048]{1,0:T(8,128)(2,1)} %copy-done, bf16[1024,1024]{1,0:T(8,128)(2,1)} %k_ref.19, bf16[1024,1024]{1,0:T(8,128)(2,1)} %v_ref.19), custom_call_target="tpu_custom_call" | custom-call | flops 1073741824 | bytes 2097152 | tf_op jit(solution)/shard_map/fwd/pallas_call | solution.py:72
  33.4 0.6 pad_add_fusion.2.scal
  34.0 4.3 %fwd.6 = (bf16[128,1024]{1,0:T(8,128)(2,1)}, f32[2,16,128]{2,1,0:T(8,128)}) custom-call(s32[1]{0:T(128)} %bitcast.2.scal, bf16[128,2048]{1,0:T(8,128)(2,1)} %copy-done.2, bf16[128,2048]{1,0:T(8,128)(2,1)} %copy-done.2, bf16[1024,1024]{1,0:T(8,128)(2,1)} %k_ref.19, bf16[1024,1024]{1,0:T(8,128)(2,1)} %v_ref.19), custom_call_target="tpu_custom_call" | custom-call | flops 1073741824 | bytes 2097152 | tf_op jit(solution)/shard_map/fwd/pallas_call | solution.py:72
  38.2 4.3 %fwd.5 = (bf16[128,1024]{1,0:T(8,128)(2,1)}, f32[2,16,128]{2,1,0:T(8,128)}) custom-call(s32[1]{0:T(128)} %bitcast.1.scal, bf16[128,2048]{1,0:T(8,128)(2,1)} %copy-done.1, bf16[128,2048]{1,0:T(8,128)(2,1)} %copy-done.1, bf16[1024,1024]{1,0:T(8,128)(2,1)} %k_ref.19, bf16[1024,1024]{1,0:T(8,128)(2,1)} %v_ref.19), custom_call_target="tpu_custom_call" | custom-call | flops 1073741824 | bytes 2097152 | tf_op jit(solution)/shard_map/fwd/pallas_call | solution.py:72
  42.5 4.3 %fwd.7 = (bf16[128,1024]{1,0:T(8,128)(2,1)}, f32[2,16,128]{2,1,0:T(8,128)}) custom-call(s32[1]{0:T(128)} %bitcast.3.scal, bf16[128,2048]{1,0:T(8,128)(2,1)} %copy-done.3, bf16[128,2048]{1,0:T(8,128)(2,1)} %copy-done.3, bf16[1024,1024]{1,0:T(8,128)(2,1)} %k_ref.19, bf16[1024,1024]{1,0:T(8,128)(2,1)} %v_ref.19), custom_call_target="tpu_custom_call" | custom-call | flops 1073741824 | bytes 2097152 | tf_op jit(solution)/shard_map/fwd/pallas_call | solution.py:72
  46.8 0.7 pad_maximum_fusion
  47.6 6.2 %all-gather = f32[32,16,128]{2,1,0:T(8,128)} all-gather(f32[8,16,128]{2,1,0:T(8,128)S(1)} %pad_maximum_fusion), channel_id=2, replica_groups=mesh['ckpt'=2,'key'=4,'qry'=4] {'key'}, dimensions={0}, use_global_device_ids=true | all-gather | bytes 327680 | tf_op jit(solution)/shard_map/all_gather | solution.py:369
  53.8 1.6 %stats.1.refs_1_.ld_ref = f32[8,8,128]{2,1,0:T(8,128)} custom-call(f32[4,8,16,128]{3,2,1,0:T(8,128)} %bitcast.10), custom_call_target="tpu_custom_call" | custom-call | flops 1048576 | bytes 524288 | tf_op jit(solution)/shard_map/stats/pallas_call | solution.py:119
  55.4 0.0 all-to-all-done.q_ref.g_ref
  55.4 0.3 collective-permute-start.9
  55.7 4.1 %dq.7 = bf16[128,1024]{1,0:T(8,128)(2,1)} custom-call(s32[1]{0:T(128)} %bitcast.3.scal, bf16[128,2048]{1,0:T(8,128)(2,1)} %copy-done.3, bf16[128,2048]{1,0:T(8,128)(2,1)} %copy-done.3, bf16[1024,1024]{1,0:T(8,128)(2,1)} %k_ref.19, bf16[1024,1024]{1,0:T(8,128)(2,1)} %v_ref.19, f32[8,8,128]{2,1,0:T(8,128)} %stats.1.refs_1_.ld_ref), custom_call_target="tpu_custom_call" | custom-call | flops 1610612736 | bytes 2097152 | tf_op jit(solution)/shard_map/dq/pallas_call | solution.py:186
  59.8 1.5 %collective-permute-start.8 = (bf16[128,1024]{1,0:T(8,128)(2,1)}, bf16[128,1024]{1,0:T(8,128)(2,1)S(1)}, u32[]{:S(2)}, u32[]{:S(2)}) collective-permute-start(bf16[128,1024]{1,0:T(8,128)(2,1)} %dq.7), channel_id=1, source_target_pairs={{0,12},{4,8},{8,4},{12,0},{1,13},{5,9},{9,5},{13,1},{2,14},{6,10},... | collective-permute-start | bytes 786440 | tf_op jit(solution)/shard_map/ppermute | solution.py:342
  61.3 4.0 %dq.6 = bf16[128,1024]{1,0:T(8,128)(2,1)} custom-call(s32[1]{0:T(128)} %bitcast.2.scal, bf16[128,2048]{1,0:T(8,128)(2,1)} %copy-done.2, bf16[128,2048]{1,0:T(8,128)(2,1)} %copy-done.2, bf16[1024,1024]{1,0:T(8,128)(2,1)} %k_ref.19, bf16[1024,1024]{1,0:T(8,128)(2,1)} %v_ref.19, f32[8,8,128]{2,1,0:T(8,128)} %stats.1.refs_1_.ld_ref), custom_call_target="tpu_custom_call" | custom-call | flops 1610612736 | bytes 2097152 | tf_op jit(solution)/shard_map/dq/pallas_call | solution.py:186
  65.3 0.6 collective-permute-start.7
  65.9 4.0 %dq.5 = bf16[128,1024]{1,0:T(8,128)(2,1)} custom-call(s32[1]{0:T(128)} %bitcast.1.scal, bf16[128,2048]{1,0:T(8,128)(2,1)} %copy-done.1, bf16[128,2048]{1,0:T(8,128)(2,1)} %copy-done.1, bf16[1024,1024]{1,0:T(8,128)(2,1)} %k_ref.19, bf16[1024,1024]{1,0:T(8,128)(2,1)} %v_ref.19, f32[8,8,128]{2,1,0:T(8,128)} %stats.1.refs_1_.ld_ref), custom_call_target="tpu_custom_call" | custom-call | flops 1610612736 | bytes 2097152 | tf_op jit(solution)/shard_map/dq/pallas_call | solution.py:186
  70.0 0.0 collective-permute-start.6
  70.0 0.7 pad_add_fusion.scal
  70.6 0.5 collective-permute-start.3
  71.1 0.0 collective-permute-done.8
  71.1 1.5 %collective-permute-start.4 = (bf16[128,1024]{1,0:T(8,128)(2,1)S(1)}, bf16[128,1024]{1,0:T(8,128)(2,1)S(1)}, u32[]{:S(2)}, u32[]{:S(2)}) collective-permute-start(bf16[128,1024]{1,0:T(8,128)(2,1)S(1)} %copy-done.12), channel_id=1, source_target_pairs={{0,8},{4,12},{8,0},{12,4},{1,9},{5,13},{9,1},{13,5},{2,10},{6,14},... | collective-permute-start | bytes 786440 | tf_op jit(solution)/shard_map/ppermute | solution.py:342
  72.6 2.0 %collective-permute-done.7 = bf16[128,1024]{1,0:T(8,128)(2,1)S(1)} collective-permute-done((bf16[128,1024]{1,0:T(8,128)(2,1)}, bf16[128,1024]{1,0:T(8,128)(2,1)S(1)}, u32[]{:S(2)}, u32[]{:S(2)}) %collective-permute-start.7) | collective-permute-done | bytes 262176 | tf_op jit(solution)/shard_map/ppermute | solution.py:342
  74.7 0.2 collective-permute-start.5
  74.9 4.0 %dq.4 = bf16[128,1024]{1,0:T(8,128)(2,1)} custom-call(s32[1]{0:T(128)} %bitcast.scal, bf16[128,2048]{1,0:T(8,128)(2,1)} %copy-done, bf16[128,2048]{1,0:T(8,128)(2,1)} %copy-done, bf16[1024,1024]{1,0:T(8,128)(2,1)} %k_ref.19, bf16[1024,1024]{1,0:T(8,128)(2,1)} %v_ref.19, f32[8,8,128]{2,1,0:T(8,128)} %stats.1.refs_1_.ld_ref), custom_call_target="tpu_custom_call" | custom-call | flops 1610612736 | bytes 2097152 | tf_op jit(solution)/shard_map/dq/pallas_call | solution.py:186
  79.0 5.1 %all-to-all-start.1 = ((f32[8,8,128]{2,1,0:T(8,128)}), f32[8,8,128]{2,1,0:T(8,128)S(1)}, u32[]{:S(2)}, u32[]{:S(2)}) async-start(f32[8,8,128]{2,1,0:T(8,128)} %stats.1.refs_1_.ld_ref), calls=%async_computation.1 | async-start | bytes 65536 | tf_op jit(solution)/shard_map/all_to_all | solution.py:372
  84.0 1.8 %add_convert_fusion = bf16[128,1024]{1,0:T(8,128)(2,1)} fusion(bf16[128,1024]{1,0:T(8,128)(2,1)S(1)} %collective-permute-done.8, bf16[128,1024]{1,0:T(8,128)(2,1)S(1)} %collective-permute-done.7, bf16[128,1024]{1,0:T(8,128)(2,1)S(1)} %collective-permute-done.6, bf16[128,1024]{1,0:T(8,128)(2,1)} %dq.4), kind=kLoop, calls=%fused_computation | loop fusion | flops 1048576 | bytes 1310720 | tf_op jit(solution)/shard_map/convert_element_type | solution.py:400
  85.9 0.0 copy-start.6
  85.9 0.7 copy-done.5
  86.6 0.1 copy-done.6
  86.7 0.1 copy-done.7
  86.8 2.7 %attn_out.1 = bf16[128,1024]{1,0:T(8,128)(2,1)} custom-call(s32[5]{0:T(128)} %stack.43.scal, f32[4,8,16,128]{3,2,1,0:T(8,128)} %bitcast.11, f32[8,8,128]{2,1,0:T(8,128)} %stats.1.refs_1_.ld_ref, bf16[128,1024]{1,0:T(8,128)(2,1)} %get-tuple-element.20.refs_2_, bf16[128,1024]{1,0:T(8,128)(2,1)} %copy-done.5, bf16[128,1024]{1,0:T(8,128)(2,1)} %copy-done.6, ...), custom_call_target="tpu_custom_call" | custom-call | flops 4194304 | bytes 2097152 | tf_op jit(solution)/shard_map/attn_out/pallas_call | solution.py:149
  89.5 0.2 all-to-all-done.1
  89.7 0.6 copy-done.8
  90.3 7.5 %dkv.2 = (bf16[1024,256]{1,0:T(8,128)(2,1)}, bf16[1024,256]{1,0:T(8,128)(2,1)}) custom-call(s32[2]{0:T(128)} %pad_add_fusion.2.scal, bf16[4,128,1024]{2,1,0:T(8,128)(2,1)} %copy-done.4, bf16[4,128,1024]{2,1,0:T(8,128)(2,1)} %copy-done.4, bf16[1024,1024]{1,0:T(8,128)(2,1)} %k_ref.19, bf16[1024,1024]{1,0:T(8,128)(2,1)} %v_ref.19, f32[4,2,8,128]{3,2,1,0:T(8,128)} %bitcast.12), custom_call_target="tpu_custom_call" | custom-call | flops 2147483648 | bytes 4194304 | tf_op jit(solution)/shard_map/dkv/pallas_call | solution.py:311
  97.8 7.5 %dkv.3 = (bf16[1024,256]{1,0:T(8,128)(2,1)}, bf16[1024,256]{1,0:T(8,128)(2,1)}) custom-call(s32[2]{0:T(128)} %pad_add_fusion.scal, bf16[4,128,1024]{2,1,0:T(8,128)(2,1)} %collective-permute-done.9.q_ref.g_ref, bf16[4,128,1024]{2,1,0:T(8,128)(2,1)} %collective-permute-done.9.q_ref.g_ref, ...), custom_call_target="tpu_custom_call", output_to_operand_aliasing={{0}: (6, {}), {1}: (7, {})} | custom-call | flops 2147483648 | bytes 4194304 | tf_op jit(solution)/shard_map/dkv/pallas_call | solution.py:311
  (28 shorter events, 0.1 us)
Async XLA Ops:
  2.6 16.9 %copy-start = (bf16[128,2048]{1,0:T(8,128)(2,1)}, bf16[128,2048]{1,0:T(8,128)(2,1)S(1)}, u32[]{:S(2)}) copy-start(bf16[128,2048]{1,0:T(8,128)(2,1)S(1)} %constant_dynamic-update-slice_fusion.q_ref.g_ref.refs_0_) | copy-start | bytes 1572868
  2.6 15.0 %collective-permute-start.1 = (bf16[128,2048]{1,0:T(8,128)(2,1)S(1)}, bf16[128,2048]{1,0:T(8,128)(2,1)S(1)}, u32[]{:S(2)}, u32[]{:S(2)}) collective-permute-start(bf16[128,2048]{1,0:T(8,128)(2,1)S(1)} %constant_dynamic-update-slice_fusion.q_ref.g_ref.refs_0_), channel_id=1, source_target_pairs={{0,8},{4,12},{8,0},{12,4},{1,9},{5,13},{9,1},{13,5},{2,10},{6,14},... | collective-permute-start | bytes 1572872 | tf_op jit(solution)/shard_map/ppermute | solution.py:342
  5.6 12.6 %collective-permute-start = (bf16[128,2048]{1,0:T(8,128)(2,1)S(1)}, bf16[128,2048]{1,0:T(8,128)(2,1)S(1)}, u32[]{:S(2)}, u32[]{:S(2)}) collective-permute-start(bf16[128,2048]{1,0:T(8,128)(2,1)S(1)} %constant_dynamic-update-slice_fusion.q_ref.g_ref.refs_0_), channel_id=1, source_target_pairs={{0,4},{4,0},{8,12},{12,8},{1,5},{5,1},{9,13},{13,9},{2,6},{6,2},{1... | collective-permute-start | bytes 1572872 | tf_op jit(solution)/shard_map/ppermute | solution.py:342
  17.5 1.9 %copy-start.2 = (bf16[128,2048]{1,0:T(8,128)(2,1)}, bf16[128,2048]{1,0:T(8,128)(2,1)S(1)}, u32[]{:S(2)}) copy-start(bf16[128,2048]{1,0:T(8,128)(2,1)S(1)} %collective-permute-done.1.q_ref.g_ref.refs_2_) | copy-start | bytes 1572868
  17.5 1.9 %collective-permute-start.2 = (bf16[128,2048]{1,0:T(8,128)(2,1)S(1)}, bf16[128,2048]{1,0:T(8,128)(2,1)S(1)}, u32[]{:S(2)}, u32[]{:S(2)}) collective-permute-start(bf16[128,2048]{1,0:T(8,128)(2,1)S(1)} %collective-permute-done.1.q_ref.g_ref.refs_2_), channel_id=1, source_target_pairs={{0,4},{4,0},{8,12},{12,8},{1,5},{5,1},{9,13},{13,9},{2,6},{6,2},{1... | collective-permute-start | bytes 1572872 | tf_op jit(solution)/shard_map/ppermute | solution.py:342
  18.2 1.2 %copy-start.1 = (bf16[128,2048]{1,0:T(8,128)(2,1)}, bf16[128,2048]{1,0:T(8,128)(2,1)S(1)}, u32[]{:S(2)}) copy-start(bf16[128,2048]{1,0:T(8,128)(2,1)S(1)} %collective-permute-done.q_ref.g_ref.refs_1_) | copy-start | bytes 1572868
  19.5 0.8 copy-start.3
  23.3 32.1 %all-to-all-start = ((bf16[4,128,1024]{2,1,0:T(8,128)(2,1)}), bf16[4,128,1024]{2,1,0:T(8,128)(2,1)S(1)}, u32[]{:S(2)}, u32[]{:S(2)}) async-start(bf16[4,128,1024]{2,1,0:T(8,128)(2,1)} %pack.1), calls=%async_computation | async-start | bytes 2097152 | tf_op jit(solution)/shard_map/all_to_all | solution.py:365
  42.5 4.3 %copy-start.9 = (f32[2,16,128]{2,1,0:T(8,128)S(1)}, f32[2,16,128]{2,1,0:T(8,128)}, u32[]{:S(2)}) copy-start(f32[2,16,128]{2,1,0:T(8,128)} %get-tuple-element.16) | copy-start | bytes 49156
  42.5 4.3 %copy-start.10 = (f32[2,16,128]{2,1,0:T(8,128)S(1)}, f32[2,16,128]{2,1,0:T(8,128)}, u32[]{:S(2)}) copy-start(f32[2,16,128]{2,1,0:T(8,128)} %get-tuple-element.18) | copy-start | bytes 49156
  42.5 4.3 %copy-start.11 = (f32[2,16,128]{2,1,0:T(8,128)S(1)}, f32[2,16,128]{2,1,0:T(8,128)}, u32[]{:S(2)}) copy-start(f32[2,16,128]{2,1,0:T(8,128)} %get-tuple-element.17) | copy-start | bytes 49156
  55.4 4.4 %copy-start.4 = (bf16[4,128,1024]{2,1,0:T(8,128)(2,1)}, bf16[4,128,1024]{2,1,0:T(8,128)(2,1)S(1)}, u32[]{:S(2)}) copy-start(bf16[4,128,1024]{2,1,0:T(8,128)(2,1)S(1)} %all-to-all-done.q_ref.g_ref) | copy-start | bytes 3145732
  55.4 42.4 %collective-permute-start.9 = (bf16[4,128,1024]{2,1,0:T(8,128)(2,1)S(1)}, bf16[4,128,1024]{2,1,0:T(8,128)(2,1)}, u32[]{:S(2)}, u32[]{:S(2)}) collective-permute-start(bf16[4,128,1024]{2,1,0:T(8,128)(2,1)S(1)} %all-to-all-done.q_ref.g_ref), channel_id=1, source_target_pairs={{0,4},{4,0},{8,12},{12,8},{1,5},{5,1},{9,13},{13,9},{2,6},{6,2},{1... | collective-permute-start | bytes 3145736 | tf_op jit(solution)/shard_map/ppermute | solution.py:342
  59.8 11.3 %collective-permute-start.8 = (bf16[128,1024]{1,0:T(8,128)(2,1)}, bf16[128,1024]{1,0:T(8,128)(2,1)S(1)}, u32[]{:S(2)}, u32[]{:S(2)}) collective-permute-start(bf16[128,1024]{1,0:T(8,128)(2,1)} %dq.7), channel_id=1, source_target_pairs={{0,12},{4,8},{8,4},{12,0},{1,13},{5,9},{9,5},{13,1},{2,14},{6,10},... | collective-permute-start | bytes 786440 | tf_op jit(solution)/shard_map/ppermute | solution.py:342
  65.3 5.3 %copy-start.14 = (bf16[128,1024]{1,0:T(8,128)(2,1)S(1)}, bf16[128,1024]{1,0:T(8,128)(2,1)}, u32[]{:S(2)}) copy-start(bf16[128,1024]{1,0:T(8,128)(2,1)} %get-tuple-element.21) | copy-start | bytes 786436
  65.3 5.8 %copy-start.12 = (bf16[128,1024]{1,0:T(8,128)(2,1)S(1)}, bf16[128,1024]{1,0:T(8,128)(2,1)}, u32[]{:S(2)}) copy-start(bf16[128,1024]{1,0:T(8,128)(2,1)} %get-tuple-element.22) | copy-start | bytes 786436
  65.3 9.4 %copy-start.13 = (bf16[128,1024]{1,0:T(8,128)(2,1)S(1)}, bf16[128,1024]{1,0:T(8,128)(2,1)}, u32[]{:S(2)}) copy-start(bf16[128,1024]{1,0:T(8,128)(2,1)} %get-tuple-element.23) | copy-start | bytes 786436
  65.3 9.4 %collective-permute-start.7 = (bf16[128,1024]{1,0:T(8,128)(2,1)}, bf16[128,1024]{1,0:T(8,128)(2,1)S(1)}, u32[]{:S(2)}, u32[]{:S(2)}) collective-permute-start(bf16[128,1024]{1,0:T(8,128)(2,1)} %dq.6), channel_id=1, source_target_pairs={{0,8},{4,12},{8,0},{12,4},{1,9},{5,13},{9,1},{13,5},{2,10},{6,14},... | collective-permute-start | bytes 786440 | tf_op jit(solution)/shard_map/ppermute | solution.py:342
  70.0 14.1 %collective-permute-start.6 = (bf16[128,1024]{1,0:T(8,128)(2,1)}, bf16[128,1024]{1,0:T(8,128)(2,1)S(1)}, u32[]{:S(2)}, u32[]{:S(2)}) collective-permute-start(bf16[128,1024]{1,0:T(8,128)(2,1)} %dq.5), channel_id=1, source_target_pairs={{0,4},{4,0},{8,12},{12,8},{1,5},{5,1},{9,13},{13,9},{2,6},{6,2},{1... | collective-permute-start | bytes 786440 | tf_op jit(solution)/shard_map/ppermute | solution.py:342
  70.6 15.2 %collective-permute-start.3 = (bf16[128,1024]{1,0:T(8,128)(2,1)S(1)}, bf16[128,1024]{1,0:T(8,128)(2,1)S(1)}, u32[]{:S(2)}, u32[]{:S(2)}) collective-permute-start(bf16[128,1024]{1,0:T(8,128)(2,1)S(1)} %copy-done.14), channel_id=1, source_target_pairs={{0,4},{4,0},{8,12},{12,8},{1,5},{5,1},{9,13},{13,9},{2,6},{6,2},{1... | collective-permute-start | bytes 786440 | tf_op jit(solution)/shard_map/ppermute | solution.py:342
  71.1 14.7 %collective-permute-start.4 = (bf16[128,1024]{1,0:T(8,128)(2,1)S(1)}, bf16[128,1024]{1,0:T(8,128)(2,1)S(1)}, u32[]{:S(2)}, u32[]{:S(2)}) collective-permute-start(bf16[128,1024]{1,0:T(8,128)(2,1)S(1)} %copy-done.12), channel_id=1, source_target_pairs={{0,8},{4,12},{8,0},{12,4},{1,9},{5,13},{9,1},{13,5},{2,10},{6,14},... | collective-permute-start | bytes 786440 | tf_op jit(solution)/shard_map/ppermute | solution.py:342
  74.7 11.2 %collective-permute-start.5 = (bf16[128,1024]{1,0:T(8,128)(2,1)S(1)}, bf16[128,1024]{1,0:T(8,128)(2,1)S(1)}, u32[]{:S(2)}, u32[]{:S(2)}) collective-permute-start(bf16[128,1024]{1,0:T(8,128)(2,1)S(1)} %copy-done.13), channel_id=1, source_target_pairs={{0,12},{4,8},{8,4},{12,0},{1,13},{5,9},{9,5},{13,1},{2,14},{6,10},... | collective-permute-start | bytes 786440 | tf_op jit(solution)/shard_map/ppermute | solution.py:342
  79.0 10.8 %all-to-all-start.1 = ((f32[8,8,128]{2,1,0:T(8,128)}), f32[8,8,128]{2,1,0:T(8,128)S(1)}, u32[]{:S(2)}, u32[]{:S(2)}) async-start(f32[8,8,128]{2,1,0:T(8,128)} %stats.1.refs_1_.ld_ref), calls=%async_computation.1 | async-start | bytes 65536 | tf_op jit(solution)/shard_map/all_to_all | solution.py:372
  85.9 0.7 copy-start.5
  85.9 0.8 copy-start.6
  85.9 0.9 copy-start.7
  89.7 0.6 copy-start.8

commit v2 on v0

v2 whole, which is shorter than its diff:
```python
import functools
import math

import jax
import jax.numpy as jnp
from jax import lax
from jax.experimental import pallas as pl
from jax.experimental.pallas import tpu as pltpu
from jax.sharding import PartitionSpec as P


HQ = 32
KVH = 8
HD = 128
GROUP = HQ // KVH
FACTOR = 1.0 / math.sqrt(HD)
SCALE2 = FACTOR * math.log2(math.e)
MIB = 1 << 20

NT = (((1,), (1,)), ((), ()))
NN = (((1,), (0,)), ((), ()))
BF16 = jnp.bfloat16
F32 = jnp.float32


VMEM = pl.BlockSpec(memory_space=pltpu.VMEM)


def call(kernel, out_shape, args, flops=1 << 20, limit=20 * MIB):
    def body(*refs):
        kernel((lax.axis_index("key"), lax.axis_index("qry")), *refs)

    return pl.pallas_call(
        body,
        in_specs=[VMEM] * len(args),
        out_specs=jax.tree.map(lambda _: VMEM, out_shape),
        out_shape=out_shape,
        cost_estimate=pl.CostEstimate(flops=flops, bytes_accessed=MIB, transcendentals=0),
        compiler_params=pltpu.CompilerParams(vmem_limit_bytes=limit),
    )(*args)


def shaped(shape, dtype):
    return jax.ShapeDtypeStruct(tuple(shape), dtype)


def dot(a, b, dims):
    return lax.dot_general(a, b, dims, preferred_element_type=F32)


def stack_heads(ref, base, count):
    return jnp.concatenate([ref[:, base + h * HD : base + (h + 1) * HD] for h in range(count)], axis=0)


def columns_of(rows):
    n, width = rows.shape
    pad = jnp.zeros((128 - n, width), F32)
    return jnp.concatenate([rows, pad], axis=0).T


def rows_of(columns, height):
    rows = columns[0].shape[0]
    lane = lax.broadcasted_iota(jnp.int32, (rows, 128), 1)
    tile = jnp.zeros((rows, 128), F32)
    for i, c in enumerate(columns):
        tile = jnp.where(lane == i, c, tile)
    return tile.T[:height]


def kv_column(scal, p, i, ups, hp):
    g = ((scal[0] ^ p) * ups + i) * hp // GROUP
    return pl.ds(pl.multiple_of(g * HD, HD), HD)


def fwd_kernel(hp, ups, places, scal, *refs):
    n = len(places)
    q_refs, (k_ref, v_ref) = refs[:n], refs[n : n + 2]
    o_refs, st_ref = refs[-n - 1 : -1], refs[-1]
    rows = q_refs[0].shape[0]
    for at, p in enumerate(places):
        for i in range(ups):
            col = kv_column(scal, p, i, ups, hp)
            base = i * hp * HD
            s = dot(stack_heads(q_refs[at], base, hp), k_ref[:, col], NT)
            m = jnp.max(s, axis=1, keepdims=True)
            e = jnp.exp2((s - m) * SCALE2)
            l = jnp.sum(e, axis=1, keepdims=True)
            o = dot(e.astype(BF16), v_ref[:, col], NN).astype(BF16)
            cols = []
            for h in range(hp):
                o_refs[at][:, base + h * HD : base + (h + 1) * HD] = o[h * rows : (h + 1) * rows]
            for x in (m, l):
                cols += [x[h * rows : (h + 1) * rows] for h in range(hp)]
            st_ref[at * ups + i] = rows_of(cols, 2 * hp)


def fwd_call(places, q, keys, values, hp, ups):
    rows, wide = q[places[0]].shape
    nk = keys.shape[0]
    out = [shaped((rows, wide), BF16)] * len(places)
    out += [shaped((len(places) * ups, 2 * hp, rows), F32)]
    res = call(
        functools.partial(fwd_kernel, hp, ups, places),
        out,
        [q[p] for p in places] + [keys, values],
        flops=4 * len(places) * rows * wide * nk,
    )
    return res[:-1], res[-1]


def delta_kernel(hp, ups, n, scal, *refs):
    o_refs, g_refs, st_refs, out_ref = refs[:n], refs[n : 2 * n], refs[2 * n : -1], refs[-1]
    for p in range(n):
        for i in range(ups):
            cols = []
            for h in range(hp):
                at = slice((i * hp + h) * HD, (i * hp + h + 1) * HD)
                product = o_refs[p][:, at].astype(F32) * g_refs[p][:, at].astype(F32)
                cols.append(jnp.sum(product, axis=1, keepdims=True))
            u = p * ups + i
            out_ref[u, : 2 * hp] = st_refs[p // 2][(p % 2) * ups + i]
            out_ref[u, 2 * hp : 3 * hp] = rows_of(cols, hp)


def stats_kernel(hp, ups, n, unit_z, scal, *refs):
    st_refs, ld_ref, z_refs = refs[:n], refs[n], refs[n + 1 :]
    for p in range(n):
        for i in range(ups):
            parts = [st_refs[q][(p ^ q) * ups + i] for q in range(n)]
            peak = parts[0][:hp]
            for x in parts[1:]:
                peak = jnp.maximum(peak, x[:hp])
            total = jnp.zeros_like(peak)
            delta = jnp.zeros_like(peak)
            for x in parts:
                w = jnp.exp2((x[:hp] - peak) * SCALE2)
                total += w * x[hp : 2 * hp]
                delta += w * x[2 * hp : 3 * hp]
            both = jnp.concatenate([peak * SCALE2 + jnp.log2(total), delta / total], axis=0)
            ld_ref[(scal[0] ^ p) * ups + i] = both
    for j, ref in enumerate(z_refs):
        ref[...] = ld_ref[pl.ds((scal[1] ^ j) * unit_z, unit_z)]


def out_kernel(hp, ups, n, scal, ld_ref, *refs):
    st_refs, parts, out_ref = refs[:n], refs[n : 2 * n], refs[2 * n]
    for i in range(ups):
        norm = ld_ref[scal[0] * ups + i][:hp]
        weights = [jnp.exp2(st_refs[q][q * ups + i][:hp] * SCALE2 - norm) for q in range(n)]
        cols = columns_of(jnp.concatenate(weights, axis=0))
        for h in range(hp):
            at = slice((i * hp + h) * HD, (i * hp + h + 1) * HD)
            total = None
            for q in range(n):
                lane = q * hp + h
                term = parts[q][:, at].astype(F32) * cols[:, lane : lane + 1]
                total = term if total is None else total + term
            out_ref[:, at] = total.astype(BF16)


def dq_kernel(hp, ups, places, scal, *refs):
    n = len(places)
    q_refs, g_refs = refs[:n], refs[n : 2 * n]
    k_ref, v_ref, ld_ref = refs[2 * n : 2 * n + 3]
    dq_refs = refs[-n:]
    rows = q_refs[0].shape[0]
    for at, p in enumerate(places):
        for i in range(ups):
            col = kv_column(scal, p, i, ups, hp)
            base = i * hp * HD
            cols = columns_of(ld_ref[(scal[0] ^ p) * ups + i])
            norm = jnp.concatenate([cols[:, h : h + 1] for h in range(hp)], axis=0)
            delta = jnp.concatenate([cols[:, hp + h : hp + h + 1] for h in range(hp)], axis=0)
            k = k_ref[:, col]
            s = dot(stack_heads(q_refs[at], base, hp), k, NT)
            e = jnp.exp2(s * SCALE2 - norm)
            gp = dot(stack_heads(g_refs[at], base, hp), v_ref[:, col], NT)
            ds = (e * (gp - delta)).astype(BF16)
            dq = (dot(ds, k, NN) * FACTOR).astype(BF16)
            for h in range(hp):
                dq_refs[at][:, base + h * HD : base + (h + 1) * HD] = dq[h * rows : (h + 1) * rows]


def dq_call(places, q, g, keys, values, ld, hp, ups):
    rows, wide = q[places[0]].shape
    return call(
        functools.partial(dq_kernel, hp, ups, places),
        [shaped((rows, wide), BF16)] * len(places),
        [q[p] for p in places] + [g[p] for p in places] + [keys, values, ld],
        flops=6 * len(places) * rows * wide * keys.shape[0],
    )


def pack_kernel(split, per_z, n, n_qry, scal, *refs):
    parts, outs = refs[: 2 * n], refs[2 * n :]
    width = parts[0].shape[1] // split
    start = pl.multiple_of((scal[0] % split) * width, HD) if split > 1 else 0
    for j in range(n_qry):
        for i in range(per_z):
            place = scal[0] ^ ((scal[1] ^ j) * per_z + i)
            for p in range(n):

                @pl.when(place == p)
                def _():
                    for kind in range(2):
                        at = (kind * per_z + i) * width
                        outs[j][:, at : at + width] = parts[kind * n + p][:, pl.ds(start, width)]


def dkv_kernel(hp, kvl, nh, n_qry, which, scal, *refs):
    qg_refs, ld_refs = refs[:n_qry], refs[n_qry : 2 * n_qry]
    k_ref, v_ref = refs[2 * n_qry : 2 * n_qry + 2]
    prior, (dk_ref, dv_ref) = refs[2 * n_qry + 2 : -2], refs[-2:]
    sub = GROUP // hp
    first = 0 if which is None else ((scal[0] % 2) ^ which) * nh
    for g in range(nh):
        col = pl.ds(pl.multiple_of((scal[1] * kvl + first + g) * HD, HD), HD)
        k, v = k_ref[:, col], v_ref[:, col]
        dk = dv = None
        for qg, ld in zip(qg_refs, ld_refs):
            base = g * GROUP * HD
            qs = stack_heads(qg, base, GROUP)
            gs = stack_heads(qg, nh * GROUP * HD + base, GROUP)
            units = [ld[(first + g) * sub + u] for u in range(sub)]
            norm = jnp.concatenate([units[h // hp][h % hp : h % hp + 1] for h in range(GROUP)], axis=1)
            delta = jnp.concatenate(
                [units[h // hp][hp + h % hp : hp + h % hp + 1] for h in range(GROUP)], axis=1
            )
            s = dot(k, qs, NT)
            e = jnp.exp2(s * SCALE2 - norm)
            gp = dot(v, gs, NT)
            ds = (e * (gp - delta)).astype(BF16)
            dv_z = dot(e.astype(BF16), gs, NN)
            dk_z = dot(ds, qs, NN)
            dv = dv_z if dv is None else dv + dv_z
            dk = dk_z if dk is None else dk + dk_z
        if which == 1:
            mine = pl.ds(pl.multiple_of((first + g) * HD, HD), HD)
        else:
            mine = pl.ds(g * HD, HD)
        dk_ref[:, mine] = (dk * FACTOR).astype(BF16)
        dv_ref[:, mine] = dv.astype(BF16)
    if which == 1:
        other = pl.ds(pl.multiple_of((scal[0] % 2) * nh * HD, HD), nh * HD)
        dk_ref[:, other] = prior[0][...]
        dv_ref[:, other] = prior[1][...]


def dkv_call(qg, keys, values, ldz, hp, kvl, which=None, prior=()):
    n_qry = len(qg)
    rows, width = qg[0].shape
    nh = width // (2 * HD * GROUP)
    nk = keys.shape[0]
    out_heads = nh if which == 0 else kvl
    return call(
        functools.partial(dkv_kernel, hp, kvl, nh, n_qry, which),
        [shaped((nk, out_heads * HD), BF16)] * 2,
        list(qg) + list(ldz) + [keys, values] + list(prior),
        flops=8 * n_qry * rows * GROUP * nh * nk * HD,
        limit=24 * MIB,
    )


def sum_kernel(scal, *refs):
    total = refs[0][...].astype(F32)
    for r in refs[1:-1]:
        total += r[...].astype(F32)
    refs[-1][...] = total.astype(BF16)


def program(queries, keys, values, out_grad):
    n_key, n_qry = lax.axis_size("key"), lax.axis_size("qry")
    rows, wide = queries.shape
    hps = HQ // n_key
    hp = min(hps, GROUP)
    ups = hps // hp
    kvl = KVH // n_qry
    per_z = n_key // n_qry
    split = 2 if (kvl % 2 == 0 and per_z == 1) else 1
    unit_z = kvl * GROUP // hp

    def swap(x, p, axis="key"):
        if p == 0:
            return x
        return lax.ppermute(x, axis, [(i, i ^ p) for i in range(lax.axis_size(axis))])

    q, g = {0: queries}, {0: out_grad}
    bit = n_key // 2
    while bit:
        for p in list(q):
            q[p ^ bit] = swap(q[p], bit)
            g[p ^ bit] = swap(g[p], bit)
        bit //= 2

    o_part, st = {}, []
    for p in range(0, n_key, 2):
        o, stat = fwd_call((p, p + 1), q, keys, values, hp, ups)
        o_part[p], o_part[p + 1] = o
        st.append(stat)
    ql, gl, ol = ([x[p] for p in range(n_key)] for x in (q, g, o_part))

    packed = call(
        functools.partial(pack_kernel, split, per_z, n_key, n_qry),
        [shaped((rows, 2 * per_z * wide // split), BF16)] * n_qry,
        ql + gl,
    )
    mine_z = [swap(x, j, "qry") for j, x in enumerate(packed)]

    own = call(
        functools.partial(delta_kernel, hp, ups, n_key),
        shaped((n_key * ups, 3 * hp, rows), F32),
        ol + gl + st,
    )
    stats = [swap(own, p) for p in range(n_key)]
    o_recv = [swap(ol[p], p) for p in range(n_key)]
    ld, *ldz = call(
        functools.partial(stats_kernel, hp, ups, n_key, unit_z),
        [shaped((n_key * ups, 2 * hp, rows), F32)] + [shaped((unit_z, 2 * hp, rows), F32)] * n_qry,
        stats,
    )
    ldz = [swap(x, j, "qry") for j, x in enumerate(ldz)]

    dq_recv = [None] * n_key
    for p in reversed(range(0, n_key, 2)):
        dqs = dq_call((p, p + 1), q, g, keys, values, ld, hp, ups)
        for at, dq in enumerate(dqs):
            dq_recv[p + at] = swap(dq, p + at)

    attn_out = call(
        functools.partial(out_kernel, hp, ups, n_key),
        shaped((rows, wide), BF16),
        [ld] + stats + o_recv,
    )

    if split == 2:
        other_z = [swap(x, 1) for x in mine_z]
        prior = dkv_call(mine_z, keys, values, ldz, hp, kvl, 0)
        key_out, value_out = dkv_call(other_z, keys, values, ldz, hp, kvl, 1, prior)
    else:
        key_out, value_out = dkv_call(mine_z, keys, values, ldz, hp, kvl)

    query_out = call(sum_kernel, shaped((rows, wide), BF16), dq_recv)
    return (attn_out, query_out, key_out, value_out)


def solution(mesh):
    in_specs = (
        P(("ckpt", "qry"), "key"),
        P(("ckpt", "key"), None),
        P(("ckpt", "key"), None),
        P(("ckpt", "qry"), "key"),
    )
    out_specs = (
        P(("ckpt", "qry"), "key"),
        P(("ckpt", "qry"), "key"),
        P(("ckpt", "key"), "qry"),
        P(("ckpt", "key"), "qry"),
    )
    return jax.shard_map(
        program, mesh=mesh, in_specs=in_specs, out_specs=out_specs, check_vma=False
    )
```

time: 262 us -> 85 us (0.32)
  the two profiles are of different devices: /device:TPU:0 before, /device:TPU:15 now
where the time goes in v2:
time: 85 us; the launch traced here: 84.8 us
  Pallas kernels  28.1 us (33%)
  waiting for transfers between devices  27.5 us (32%)
  starting transfers between devices  24.2 us (28%)
  local copies, waits for them, and re-layouts  4.15 us (5%)
    pallas_call x11, Pallas kernels, call(): pl.pallas_call(body, in_specs=[VMEM] * len(args), out_specs=jax.tree.map(...  28.1 us
    ppermute x25, waiting for transfers between devices, swap(): lax.ppermute(x, axis, [(i, i ^ p) for i in range(lax.axis_size(axis))])  27.5 us
    ppermute x25, starting transfers between devices, swap(): lax.ppermute(x, axis, [(i, i ^ p) for i in range(lax.axis_size(axis))])  24.2 us
    unnamed x14, local copies, waits for them, and re-layouts  4.15 us
  transfers between devices with their start and end apart: 25, of which 6 were waited for; matrix products, arithmetic and copies ran while one was open for 0% of the time, Pallas kernels for 27%

profile of v2, /device:TPU:15, one launch (start us, length us, event | category | flops | bytes accessed | tf_op | source)
XLA Modules:
  0.0 84.8 jit_solution(16107280179702221068)
XLA Ops:
  0.6 0.3 collective-permute-start.1
  1.0 1.2 %collective-permute-start.4 = (bf16[128,1024]{1,0:T(8,128)(2,1)}, bf16[128,1024]{1,0:T(8,128)(2,1)S(1)}, u32[]{:S(2)}, u32[]{:S(2)}) collective-permute-start(bf16[128,1024]{1,0:T(8,128)(2,1)} %refs_4_.7), channel_id=1, source_target_pairs={{0,8},{4,12},{8,0},{12,4},{1,9},{5,13},{9,1},{13,5},{2,10},{6,14},... | collective-permute-start | bytes 786440 | tf_op jit(solution)/shard_map/ppermute | solution.py:285
  2.2 1.2 %collective-permute-start = (bf16[128,1024]{1,0:T(8,128)(2,1)}, bf16[128,1024]{1,0:T(8,128)(2,1)S(1)}, u32[]{:S(2)}, u32[]{:S(2)}) collective-permute-start(bf16[128,1024]{1,0:T(8,128)(2,1)} %refs_0_.5), channel_id=1, source_target_pairs={{0,4},{4,0},{8,12},{12,8},{1,5},{5,1},{9,13},{13,9},{2,6},{6,2},{1... | collective-permute-start | bytes 786440 | tf_op jit(solution)/shard_map/ppermute | solution.py:285
  3.4 4.7 %collective-permute-done.1.refs_0_.refs_2_ = bf16[128,1024]{1,0:T(8,128)(2,1)S(1)} collective-permute-done((bf16[128,1024]{1,0:T(8,128)(2,1)}, bf16[128,1024]{1,0:T(8,128)(2,1)S(1)}, u32[]{:S(2)}, u32[]{:S(2)}) %collective-permute-start.1) | collective-permute-done | bytes 262176 | tf_op jit(solution)/shard_map/ppermute | solution.py:285
  8.1 2.7 %collective-permute-start.2 = (bf16[128,1024]{1,0:T(8,128)(2,1)S(1)}, bf16[128,1024]{1,0:T(8,128)(2,1)S(1)}, u32[]{:S(2)}, u32[]{:S(2)}) collective-permute-start(bf16[128,1024]{1,0:T(8,128)(2,1)S(1)} %collective-permute-done.1.refs_0_.refs_2_), channel_id=1, source_target_pairs={{0,4},{4,0},{8,12},{12,8},{1,5},{5,1},{9,13},{13,9},{2,6},{6,2},{1... | collective-permute-start | bytes 786440 | tf_op jit(solution)/shard_map/ppermute | solution.py:285
  10.8 0.0 collective-permute-start.3
  10.8 3.0 %collective-permute-done.4.refs_6_.refs_2_ = bf16[128,1024]{1,0:T(8,128)(2,1)S(1)} collective-permute-done((bf16[128,1024]{1,0:T(8,128)(2,1)}, bf16[128,1024]{1,0:T(8,128)(2,1)S(1)}, u32[]{:S(2)}, u32[]{:S(2)}) %collective-permute-start.4) | collective-permute-done | bytes 262176 | tf_op jit(solution)/shard_map/ppermute | solution.py:285
  13.7 1.5 %collective-permute-start.5 = (bf16[128,1024]{1,0:T(8,128)(2,1)S(1)}, bf16[128,1024]{1,0:T(8,128)(2,1)S(1)}, u32[]{:S(2)}, u32[]{:S(2)}) collective-permute-start(bf16[128,1024]{1,0:T(8,128)(2,1)S(1)} %collective-permute-done.4.refs_6_.refs_2_), channel_id=1, source_target_pairs={{0,4},{4,0},{8,12},{12,8},{1,5},{5,1},{9,13},{13,9},{2,6},{6,2},{1... | collective-permute-start | bytes 786440 | tf_op jit(solution)/shard_map/ppermute | solution.py:285
  15.2 0.0 collective-permute-done.refs_1_
  15.3 1.6 %copy-done = bf16[1024,1024]{1,0:T(8,128)(2,1)S(1)} copy-done((bf16[1024,1024]{1,0:T(8,128)(2,1)S(1)}, bf16[1024,1024]{1,0:T(8,128)(2,1)}, u32[]{:S(2)}) %copy-start) | copy-done | bytes 2097176
  16.8 1.6 %copy-done.2 = bf16[1024,1024]{1,0:T(8,128)(2,1)S(1)} copy-done((bf16[1024,1024]{1,0:T(8,128)(2,1)S(1)}, bf16[1024,1024]{1,0:T(8,128)(2,1)}, u32[]{:S(2)}) %copy-start.2) | copy-done | bytes 2097176
  18.4 0.9 %copy-done.4 = bf16[128,1024]{1,0:T(8,128)(2,1)S(1)} copy-done((bf16[128,1024]{1,0:T(8,128)(2,1)S(1)}, bf16[128,1024]{1,0:T(8,128)(2,1)}, u32[]{:S(2)}) %copy-start.4) | copy-done | bytes 262168
  19.4 3.2 %shard_map.75 = (bf16[128,1024]{1,0:T(8,128)(2,1)S(1)}, bf16[128,1024]{1,0:T(8,128)(2,1)S(1)}, f32[4,8,128]{2,1,0:T(8,128)S(1)}) custom-call(bf16[128,1024]{1,0:T(8,128)(2,1)S(1)} %copy-done.4, bf16[128,1024]{1,0:T(8,128)(2,1)S(1)} %collective-permute-done.refs_1_, bf16[1024,1024]{1,0:T(8,128)(2,1)S(1)} %copy-done, bf16[1024,1024]{1,0:T(8,128)(2,1)S(1)} %copy-done.2), custom_call_target="tpu_custom_call" | custom-call | flops 1073741824 | bytes 1048576 | tf_op jit(solution)/shard_map/pallas_call | solution.py:33
  22.6 0.0 copy-start.6
  22.6 0.1 collective-permute-start.9
  22.7 3.2 %shard_map.76 = (bf16[128,1024]{1,0:T(8,128)(2,1)S(1)}, bf16[128,1024]{1,0:T(8,128)(2,1)S(1)}, f32[4,8,128]{2,1,0:T(8,128)S(1)}) custom-call(bf16[128,1024]{1,0:T(8,128)(2,1)S(1)} %collective-permute-done.1.refs_0_.refs_2_, bf16[128,1024]{1,0:T(8,128)(2,1)S(1)} %collective-permute-done.2.refs_1_.refs_3_, bf16[1024,1024]{1,0:T(8,128)(2,1)S(1)} %copy-done.1, ...), custom_call_target="tpu_custom_call" | custom-call | flops 1073741824 | bytes 1048576 | tf_op jit(solution)/shard_map/pallas_call | solution.py:33
  25.9 0.0 copy-start.5
  26.0 0.8 shard_map.77.refs_0_.refs_1_
  26.8 0.5 collective-permute-start.6
  27.3 0.2 collective-permute-start.7
  27.5 1.5 %collective-permute-start.8 = (f32[8,12,128]{2,1,0:T(8,128)S(1)}, f32[8,12,128]{2,1,0:T(8,128)S(1)}, u32[]{:S(2)}, u32[]{:S(2)}) collective-permute-start(f32[8,12,128]{2,1,0:T(8,128)S(1)} %shard_map.77.refs_0_.refs_1_), channel_id=1, source_target_pairs={{0,12},{4,8},{8,4},{12,0},{1,13},{5,9},{9,5},{13,1},{2,14},{6,10},... | collective-permute-start | bytes 147464 | tf_op jit(solution)/shard_map/ppermute | solution.py:285
  29.0 0.2 collective-permute-start.10
  29.2 0.3 shard_map.83
  29.6 1.6 %collective-permute-start.11 = (bf16[128,1024]{1,0:T(8,128)(2,1)S(1)}, bf16[128,1024]{1,0:T(8,128)(2,1)S(1)}, u32[]{:S(2)}, u32[]{:S(2)}) collective-permute-start(bf16[128,1024]{1,0:T(8,128)(2,1)S(1)} %get-tuple-element.30.refs_3_), channel_id=1, source_target_pairs={{0,12},{4,8},{8,4},{12,0},{1,13},{5,9},{9,5},{13,1},{2,14},{6,10},... | collective-permute-start | bytes 786440 | tf_op jit(solution)/shard_map/ppermute | solution.py:285
  31.2 1.9 %collective-permute-done.8.refs_3_.refs_4_ = f32[8,12,128]{2,1,0:T(8,128)S(1)} collective-permute-done((f32[8,12,128]{2,1,0:T(8,128)S(1)}, f32[8,12,128]{2,1,0:T(8,128)S(1)}, u32[]{:S(2)}, u32[]{:S(2)}) %collective-permute-start.8) | collective-permute-done | bytes 49184 | tf_op jit(solution)/shard_map/ppermute | solution.py:285
  33.1 0.1 shard_map.78
  33.1 0.2 collective-permute-start.22
  33.4 2.3 %collective-permute-start.23 = (f32[2,8,128]{2,1,0:T(8,128)S(1)}, f32[2,8,128]{2,1,0:T(8,128)S(1)}, u32[]{:S(2)}, u32[]{:S(2)}) collective-permute-start(f32[2,8,128]{2,1,0:T(8,128)S(1)} %get-tuple-element.44), channel_id=1, source_target_pairs={{0,2},{1,3},{2,0},{3,1},{4,6},{5,7},{6,4},{7,5},{8,10},{9,11},{10,... | collective-permute-start | bytes 24584 | tf_op jit(solution)/shard_map/ppermute | solution.py:285
  35.7 4.0 %shard_map.80 = (bf16[128,1024]{1,0:T(8,128)(2,1)S(1)}, bf16[128,1024]{1,0:T(8,128)(2,1)S(1)}) custom-call(bf16[128,1024]{1,0:T(8,128)(2,1)S(1)} %copy-done.5, bf16[128,1024]{1,0:T(8,128)(2,1)S(1)} %collective-permute-done.refs_1_, bf16[128,1024]{1,0:T(8,128)(2,1)S(1)} %copy-done.6, bf16[128,1024]{1,0:T(8,128)(2,1)S(1)} %collective-permute-done.3.refs_5_.refs_3_, ...), custom_call_target="tpu_custom_call" | custom-call | flops 1610612736 | bytes 1048576 | tf_op jit(solution)/shard_map/pallas_call | solution.py:33
  39.7 0.2 collective-permute-start.24
  39.9 3.9 %shard_map.81 = (bf16[128,1024]{1,0:T(8,128)(2,1)S(1)}, bf16[128,1024]{1,0:T(8,128)(2,1)S(1)}) custom-call(bf16[128,1024]{1,0:T(8,128)(2,1)S(1)} %collective-permute-done.1.refs_0_.refs_2_, bf16[128,1024]{1,0:T(8,128)(2,1)S(1)} %collective-permute-done.2.refs_1_.refs_3_, bf16[128,1024]{1,0:T(8,128)(2,1)S(1)} %collective-permute-done.4.refs_6_.refs_2_, ...), custom_call_target="tpu_custom_call" | custom-call | flops 1610612736 | bytes 1048576 | tf_op jit(solution)/shard_map/pallas_call | solution.py:33
  43.9 1.2 %collective-permute-start.16 = (bf16[128,1024]{1,0:T(8,128)(2,1)S(1)}, bf16[128,1024]{1,0:T(8,128)(2,1)S(1)}, u32[]{:S(2)}, u32[]{:S(2)}) collective-permute-start(bf16[128,1024]{1,0:T(8,128)(2,1)S(1)} %get-tuple-element.39), channel_id=1, source_target_pairs={{0,1},{1,0},{2,3},{3,2},{4,5},{5,4},{6,7},{7,6},{8,9},{9,8},{10,11... | collective-permute-start | bytes 786440 | tf_op jit(solution)/shard_map/ppermute | solution.py:285
  45.1 2.1 %collective-permute-start.18 = (bf16[128,1024]{1,0:T(8,128)(2,1)S(1)}, bf16[128,1024]{1,0:T(8,128)(2,1)S(1)}, u32[]{:S(2)}, u32[]{:S(2)}) collective-permute-start(bf16[128,1024]{1,0:T(8,128)(2,1)S(1)} %get-tuple-element.40), channel_id=1, source_target_pairs={{0,2},{1,3},{2,0},{3,1},{4,6},{5,7},{6,4},{7,5},{8,10},{9,11},{10,... | collective-permute-start | bytes 786440 | tf_op jit(solution)/shard_map/ppermute | solution.py:285
  47.2 0.3 collective-permute-start.20
  47.5 1.0 %collective-permute-start.12 = (bf16[128,1024]{1,0:T(8,128)(2,1)S(1)}, bf16[128,1024]{1,0:T(8,128)(2,1)S(1)}, u32[]{:S(2)}, u32[]{:S(2)}) collective-permute-start(bf16[128,1024]{1,0:T(8,128)(2,1)S(1)} %get-tuple-element.35), channel_id=1, source_target_pairs={{0,4},{4,0},{8,12},{12,8},{1,5},{5,1},{9,13},{13,9},{2,6},{6,2},{1... | collective-permute-start | bytes 786440 | tf_op jit(solution)/shard_map/ppermute | solution.py:285
  48.5 0.5 collective-permute-start.13
  49.0 6.4 %collective-permute-done.16.refs_1_ = bf16[128,1024]{1,0:T(8,128)(2,1)S(1)} collective-permute-done((bf16[128,1024]{1,0:T(8,128)(2,1)S(1)}, bf16[128,1024]{1,0:T(8,128)(2,1)S(1)}, u32[]{:S(2)}, u32[]{:S(2)}) %collective-permute-start.16) | collective-permute-done | bytes 262176 | tf_op jit(solution)/shard_map/ppermute | solution.py:285
  55.4 1.0 %collective-permute-start.14 = (bf16[128,1024]{1,0:T(8,128)(2,1)S(1)}, bf16[128,1024]{1,0:T(8,128)(2,1)S(1)}, u32[]{:S(2)}, u32[]{:S(2)}) collective-permute-start(bf16[128,1024]{1,0:T(8,128)(2,1)S(1)} %get-tuple-element.37), channel_id=1, source_target_pairs={{0,12},{4,8},{8,4},{12,0},{1,13},{5,9},{9,5},{13,1},{2,14},{6,10},... | collective-permute-start | bytes 786440 | tf_op jit(solution)/shard_map/ppermute | solution.py:285
  56.4 7.3 %collective-permute-done.18.refs_2_ = bf16[128,1024]{1,0:T(8,128)(2,1)S(1)} collective-permute-done((bf16[128,1024]{1,0:T(8,128)(2,1)S(1)}, bf16[128,1024]{1,0:T(8,128)(2,1)S(1)}, u32[]{:S(2)}, u32[]{:S(2)}) %collective-permute-start.18) | collective-permute-done | bytes 262176 | tf_op jit(solution)/shard_map/ppermute | solution.py:285
  63.7 2.3 %collective-permute-start.15 = (bf16[128,1024]{1,0:T(8,128)(2,1)S(1)}, bf16[128,1024]{1,0:T(8,128)(2,1)S(1)}, u32[]{:S(2)}, u32[]{:S(2)}) collective-permute-start(bf16[128,1024]{1,0:T(8,128)(2,1)S(1)} %get-tuple-element.38.refs_0_), channel_id=1, source_target_pairs={{0,4},{4,0},{8,12},{12,8},{1,5},{5,1},{9,13},{13,9},{2,6},{6,2},{1... | collective-permute-start | bytes 786440 | tf_op jit(solution)/shard_map/ppermute | solution.py:285
  66.0 4.3 %collective-permute-done.20.refs_3_ = bf16[128,1024]{1,0:T(8,128)(2,1)S(1)} collective-permute-done((bf16[128,1024]{1,0:T(8,128)(2,1)S(1)}, bf16[128,1024]{1,0:T(8,128)(2,1)S(1)}, u32[]{:S(2)}, u32[]{:S(2)}) %collective-permute-start.20) | collective-permute-done | bytes 262176 | tf_op jit(solution)/shard_map/ppermute | solution.py:285
  70.2 1.3 %collective-permute-start.17 = (bf16[128,1024]{1,0:T(8,128)(2,1)S(1)}, bf16[128,1024]{1,0:T(8,128)(2,1)S(1)}, u32[]{:S(2)}, u32[]{:S(2)}) collective-permute-start(bf16[128,1024]{1,0:T(8,128)(2,1)S(1)} %collective-permute-done.16.refs_1_), channel_id=1, source_target_pairs={{0,4},{4,0},{8,12},{12,8},{1,5},{5,1},{9,13},{13,9},{2,6},{6,2},{1... | collective-permute-start | bytes 786440 | tf_op jit(solution)/shard_map/ppermute | solution.py:285
  71.6 0.0 collective-permute-start.19
  71.6 0.5 collective-permute-start.21
  72.1 1.5 %shard_map.79 = bf16[128,1024]{1,0:T(8,128)(2,1)} custom-call(f32[8,8,128]{2,1,0:T(8,128)S(1)} %get-tuple-element.33.refs_0_.refs_6_, f32[8,12,128]{2,1,0:T(8,128)S(1)} %shard_map.77.refs_0_.refs_1_, f32[8,12,128]{2,1,0:T(8,128)S(1)} %collective-permute-done.6.refs_1_.refs_2_, f32[8,12,128]{2,1,0:T(8,128)S(1)} %collective-permute-done.7.refs_2_.refs_3_, ...), custom_call_target="tpu_custom_call" | custom-call | flops 1048576 | bytes 1048576 | tf_op jit(solution)/shard_map/pallas_call | solution.py:33
  73.6 4.8 %shard_map.84 = (bf16[1024,128]{1,0:T(8,128)(2,1)S(1)}, bf16[1024,128]{1,0:T(8,128)(2,1)S(1)}) custom-call(bf16[128,1024]{1,0:T(8,128)(2,1)S(1)} %get-tuple-element.38.refs_0_, bf16[128,1024]{1,0:T(8,128)(2,1)S(1)} %collective-permute-done.16.refs_1_, bf16[128,1024]{1,0:T(8,128)(2,1)S(1)} %collective-permute-done.18.refs_2_, ...), custom_call_target="tpu_custom_call" | custom-call | flops 2147483648 | bytes 1048576 | tf_op jit(solution)/shard_map/pallas_call | solution.py:33
  78.3 0.8 shard_map.82
  79.2 5.6 %shard_map.85 = (bf16[1024,256]{1,0:T(8,128)(2,1)}, bf16[1024,256]{1,0:T(8,128)(2,1)}) custom-call(bf16[128,1024]{1,0:T(8,128)(2,1)S(1)} %collective-permute-done.15.refs_0_, bf16[128,1024]{1,0:T(8,128)(2,1)S(1)} %collective-permute-done.17.refs_1_, bf16[128,1024]{1,0:T(8,128)(2,1)S(1)} %collective-permute-done.19.refs_2_, ...), custom_call_target="tpu_custom_call" | custom-call | flops 2147483648 | bytes 1048576 | tf_op jit(solution)/shard_map/pallas_call | solution.py:33
  (27 shorter events, 0.1 us)
Async XLA Ops:
  0.6 7.5 %collective-permute-start.1 = (bf16[128,1024]{1,0:T(8,128)(2,1)}, bf16[128,1024]{1,0:T(8,128)(2,1)S(1)}, u32[]{:S(2)}, u32[]{:S(2)}) collective-permute-start(bf16[128,1024]{1,0:T(8,128)(2,1)} %refs_0_.5), channel_id=1, source_target_pairs={{0,8},{4,12},{8,0},{12,4},{1,9},{5,13},{9,1},{13,5},{2,10},{6,14},... | collective-permute-start | bytes 786440 | tf_op jit(solution)/shard_map/ppermute | solution.py:285
  1.0 12.8 %collective-permute-start.4 = (bf16[128,1024]{1,0:T(8,128)(2,1)}, bf16[128,1024]{1,0:T(8,128)(2,1)S(1)}, u32[]{:S(2)}, u32[]{:S(2)}) collective-permute-start(bf16[128,1024]{1,0:T(8,128)(2,1)} %refs_4_.7), channel_id=1, source_target_pairs={{0,8},{4,12},{8,0},{12,4},{1,9},{5,13},{9,1},{13,5},{2,10},{6,14},... | collective-permute-start | bytes 786440 | tf_op jit(solution)/shard_map/ppermute | solution.py:285
  2.2 13.1 %collective-permute-start = (bf16[128,1024]{1,0:T(8,128)(2,1)}, bf16[128,1024]{1,0:T(8,128)(2,1)S(1)}, u32[]{:S(2)}, u32[]{:S(2)}) collective-permute-start(bf16[128,1024]{1,0:T(8,128)(2,1)} %refs_0_.5), channel_id=1, source_target_pairs={{0,4},{4,0},{8,12},{12,8},{1,5},{5,1},{9,13},{13,9},{2,6},{6,2},{1... | collective-permute-start | bytes 786440 | tf_op jit(solution)/shard_map/ppermute | solution.py:285
  8.1 14.6 %collective-permute-start.2 = (bf16[128,1024]{1,0:T(8,128)(2,1)S(1)}, bf16[128,1024]{1,0:T(8,128)(2,1)S(1)}, u32[]{:S(2)}, u32[]{:S(2)}) collective-permute-start(bf16[128,1024]{1,0:T(8,128)(2,1)S(1)} %collective-permute-done.1.refs_0_.refs_2_), channel_id=1, source_target_pairs={{0,4},{4,0},{8,12},{12,8},{1,5},{5,1},{9,13},{13,9},{2,6},{6,2},{1... | collective-permute-start | bytes 786440 | tf_op jit(solution)/shard_map/ppermute | solution.py:285
  10.8 15.2 %collective-permute-start.3 = (bf16[128,1024]{1,0:T(8,128)(2,1)}, bf16[128,1024]{1,0:T(8,128)(2,1)S(1)}, u32[]{:S(2)}, u32[]{:S(2)}) collective-permute-start(bf16[128,1024]{1,0:T(8,128)(2,1)} %refs_4_.7), channel_id=1, source_target_pairs={{0,4},{4,0},{8,12},{12,8},{1,5},{5,1},{9,13},{13,9},{2,6},{6,2},{1... | collective-permute-start | bytes 786440 | tf_op jit(solution)/shard_map/ppermute | solution.py:285
  13.7 12.2 %collective-permute-start.5 = (bf16[128,1024]{1,0:T(8,128)(2,1)S(1)}, bf16[128,1024]{1,0:T(8,128)(2,1)S(1)}, u32[]{:S(2)}, u32[]{:S(2)}) collective-permute-start(bf16[128,1024]{1,0:T(8,128)(2,1)S(1)} %collective-permute-done.4.refs_6_.refs_2_), channel_id=1, source_target_pairs={{0,4},{4,0},{8,12},{12,8},{1,5},{5,1},{9,13},{13,9},{2,6},{6,2},{1... | collective-permute-start | bytes 786440 | tf_op jit(solution)/shard_map/ppermute | solution.py:285
  15.2 1.6 %copy-start = (bf16[1024,1024]{1,0:T(8,128)(2,1)S(1)}, bf16[1024,1024]{1,0:T(8,128)(2,1)}, u32[]{:S(2)}) copy-start(bf16[1024,1024]{1,0:T(8,128)(2,1)} %refs_8_.3) | copy-start | bytes 6291460
  16.8 1.6 %copy-start.2 = (bf16[1024,1024]{1,0:T(8,128)(2,1)S(1)}, bf16[1024,1024]{1,0:T(8,128)(2,1)}, u32[]{:S(2)}) copy-start(bf16[1024,1024]{1,0:T(8,128)(2,1)} %refs_9_.3) | copy-start | bytes 6291460
  18.4 0.9 %copy-start.4 = (bf16[128,1024]{1,0:T(8,128)(2,1)S(1)}, bf16[128,1024]{1,0:T(8,128)(2,1)}, u32[]{:S(2)}) copy-start(bf16[128,1024]{1,0:T(8,128)(2,1)} %refs_0_.5) | copy-start | bytes 786436
  19.4 3.3 %copy-start.1 = (bf16[1024,1024]{1,0:T(8,128)(2,1)S(1)}, bf16[1024,1024]{1,0:T(8,128)(2,1)}, u32[]{:S(2)}) copy-start(bf16[1024,1024]{1,0:T(8,128)(2,1)} %refs_8_.3) | copy-start | bytes 6291460
  19.4 3.3 %copy-start.3 = (bf16[1024,1024]{1,0:T(8,128)(2,1)S(1)}, bf16[1024,1024]{1,0:T(8,128)(2,1)}, u32[]{:S(2)}) copy-start(bf16[1024,1024]{1,0:T(8,128)(2,1)} %refs_9_.3) | copy-start | bytes 6291460
  22.6 3.3 %copy-start.6 = (bf16[128,1024]{1,0:T(8,128)(2,1)S(1)}, bf16[128,1024]{1,0:T(8,128)(2,1)}, u32[]{:S(2)}) copy-start(bf16[128,1024]{1,0:T(8,128)(2,1)} %refs_4_.7) | copy-start | bytes 786436
  22.6 17.0 %collective-permute-start.9 = (bf16[128,1024]{1,0:T(8,128)(2,1)S(1)}, bf16[128,1024]{1,0:T(8,128)(2,1)S(1)}, u32[]{:S(2)}, u32[]{:S(2)}) collective-permute-start(bf16[128,1024]{1,0:T(8,128)(2,1)S(1)} %get-tuple-element.28.refs_1_), channel_id=1, source_target_pairs={{0,4},{4,0},{8,12},{12,8},{1,5},{5,1},{9,13},{13,9},{2,6},{6,2},{1... | collective-permute-start | bytes 786440 | tf_op jit(solution)/shard_map/ppermute | solution.py:285
  25.9 9.7 %copy-start.5 = (bf16[128,1024]{1,0:T(8,128)(2,1)S(1)}, bf16[128,1024]{1,0:T(8,128)(2,1)}, u32[]{:S(2)}) copy-start(bf16[128,1024]{1,0:T(8,128)(2,1)} %refs_0_.5) | copy-start | bytes 786436
  26.8 2.8 %collective-permute-start.6 = (f32[8,12,128]{2,1,0:T(8,128)S(1)}, f32[8,12,128]{2,1,0:T(8,128)S(1)}, u32[]{:S(2)}, u32[]{:S(2)}) collective-permute-start(f32[8,12,128]{2,1,0:T(8,128)S(1)} %shard_map.77.refs_0_.refs_1_), channel_id=1, source_target_pairs={{0,4},{4,0},{8,12},{12,8},{1,5},{5,1},{9,13},{13,9},{2,6},{6,2},{1... | collective-permute-start | bytes 147464 | tf_op jit(solution)/shard_map/ppermute | solution.py:285
  27.3 3.9 %collective-permute-start.7 = (f32[8,12,128]{2,1,0:T(8,128)S(1)}, f32[8,12,128]{2,1,0:T(8,128)S(1)}, u32[]{:S(2)}, u32[]{:S(2)}) collective-permute-start(f32[8,12,128]{2,1,0:T(8,128)S(1)} %shard_map.77.refs_0_.refs_1_), channel_id=1, source_target_pairs={{0,8},{4,12},{8,0},{12,4},{1,9},{5,13},{9,1},{13,5},{2,10},{6,14},... | collective-permute-start | bytes 147464 | tf_op jit(solution)/shard_map/ppermute | solution.py:285
  27.5 5.5 %collective-permute-start.8 = (f32[8,12,128]{2,1,0:T(8,128)S(1)}, f32[8,12,128]{2,1,0:T(8,128)S(1)}, u32[]{:S(2)}, u32[]{:S(2)}) collective-permute-start(f32[8,12,128]{2,1,0:T(8,128)S(1)} %shard_map.77.refs_0_.refs_1_), channel_id=1, source_target_pairs={{0,12},{4,8},{8,4},{12,0},{1,13},{5,9},{9,5},{13,1},{2,14},{6,10},... | collective-permute-start | bytes 147464 | tf_op jit(solution)/shard_map/ppermute | solution.py:285
  29.0 18.5 %collective-permute-start.10 = (bf16[128,1024]{1,0:T(8,128)(2,1)S(1)}, bf16[128,1024]{1,0:T(8,128)(2,1)S(1)}, u32[]{:S(2)}, u32[]{:S(2)}) collective-permute-start(bf16[128,1024]{1,0:T(8,128)(2,1)S(1)} %get-tuple-element.29.refs_2_), channel_id=1, source_target_pairs={{0,8},{4,12},{8,0},{12,4},{1,9},{5,13},{9,1},{13,5},{2,10},{6,14},... | collective-permute-start | bytes 786440 | tf_op jit(solution)/shard_map/ppermute | solution.py:285
  29.6 19.0 %collective-permute-start.11 = (bf16[128,1024]{1,0:T(8,128)(2,1)S(1)}, bf16[128,1024]{1,0:T(8,128)(2,1)S(1)}, u32[]{:S(2)}, u32[]{:S(2)}) collective-permute-start(bf16[128,1024]{1,0:T(8,128)(2,1)S(1)} %get-tuple-element.30.refs_3_), channel_id=1, source_target_pairs={{0,12},{4,8},{8,4},{12,0},{1,13},{5,9},{9,5},{13,1},{2,14},{6,10},... | collective-permute-start | bytes 786440 | tf_op jit(solution)/shard_map/ppermute | solution.py:285
  33.1 10.7 %collective-permute-start.22 = (f32[2,8,128]{2,1,0:T(8,128)S(1)}, f32[2,8,128]{2,1,0:T(8,128)S(1)}, u32[]{:S(2)}, u32[]{:S(2)}) collective-permute-start(f32[2,8,128]{2,1,0:T(8,128)S(1)} %get-tuple-element.43), channel_id=1, source_target_pairs={{0,1},{1,0},{2,3},{3,2},{4,5},{5,4},{6,7},{7,6},{8,9},{9,8},{10,11... | collective-permute-start | bytes 24584 | tf_op jit(solution)/shard_map/ppermute | solution.py:285
  33.4 11.7 %collective-permute-start.23 = (f32[2,8,128]{2,1,0:T(8,128)S(1)}, f32[2,8,128]{2,1,0:T(8,128)S(1)}, u32[]{:S(2)}, u32[]{:S(2)}) collective-permute-start(f32[2,8,128]{2,1,0:T(8,128)S(1)} %get-tuple-element.44), channel_id=1, source_target_pairs={{0,2},{1,3},{2,0},{3,1},{4,6},{5,7},{6,4},{7,5},{8,10},{9,11},{10,... | collective-permute-start | bytes 24584 | tf_op jit(solution)/shard_map/ppermute | solution.py:285
  39.7 7.6 %collective-permute-start.24 = (f32[2,8,128]{2,1,0:T(8,128)S(1)}, f32[2,8,128]{2,1,0:T(8,128)S(1)}, u32[]{:S(2)}, u32[]{:S(2)}) collective-permute-start(f32[2,8,128]{2,1,0:T(8,128)S(1)} %get-tuple-element.45), channel_id=1, source_target_pairs={{0,3},{1,2},{2,1},{3,0},{4,7},{5,6},{6,5},{7,4},{8,11},{9,10},{10,... | collective-permute-start | bytes 24584 | tf_op jit(solution)/shard_map/ppermute | solution.py:285
  43.9 11.5 %collective-permute-start.16 = (bf16[128,1024]{1,0:T(8,128)(2,1)S(1)}, bf16[128,1024]{1,0:T(8,128)(2,1)S(1)}, u32[]{:S(2)}, u32[]{:S(2)}) collective-permute-start(bf16[128,1024]{1,0:T(8,128)(2,1)S(1)} %get-tuple-element.39), channel_id=1, source_target_pairs={{0,1},{1,0},{2,3},{3,2},{4,5},{5,4},{6,7},{7,6},{8,9},{9,8},{10,11... | collective-permute-start | bytes 786440 | tf_op jit(solution)/shard_map/ppermute | solution.py:285
  45.1 18.6 %collective-permute-start.18 = (bf16[128,1024]{1,0:T(8,128)(2,1)S(1)}, bf16[128,1024]{1,0:T(8,128)(2,1)S(1)}, u32[]{:S(2)}, u32[]{:S(2)}) collective-permute-start(bf16[128,1024]{1,0:T(8,128)(2,1)S(1)} %get-tuple-element.40), channel_id=1, source_target_pairs={{0,2},{1,3},{2,0},{3,1},{4,6},{5,7},{6,4},{7,5},{8,10},{9,11},{10,... | collective-permute-start | bytes 786440 | tf_op jit(solution)/shard_map/ppermute | solution.py:285
  47.2 23.0 %collective-permute-start.20 = (bf16[128,1024]{1,0:T(8,128)(2,1)S(1)}, bf16[128,1024]{1,0:T(8,128)(2,1)S(1)}, u32[]{:S(2)}, u32[]{:S(2)}) collective-permute-start(bf16[128,1024]{1,0:T(8,128)(2,1)S(1)} %get-tuple-element.41), channel_id=1, source_target_pairs={{0,3},{1,2},{2,1},{3,0},{4,7},{5,6},{6,5},{7,4},{8,11},{9,10},{10,... | collective-permute-start | bytes 786440 | tf_op jit(solution)/shard_map/ppermute | solution.py:285
  47.5 24.1 %collective-permute-start.12 = (bf16[128,1024]{1,0:T(8,128)(2,1)S(1)}, bf16[128,1024]{1,0:T(8,128)(2,1)S(1)}, u32[]{:S(2)}, u32[]{:S(2)}) collective-permute-start(bf16[128,1024]{1,0:T(8,128)(2,1)S(1)} %get-tuple-element.35), channel_id=1, source_target_pairs={{0,4},{4,0},{8,12},{12,8},{1,5},{5,1},{9,13},{13,9},{2,6},{6,2},{1... | collective-permute-start | bytes 786440 | tf_op jit(solution)/shard_map/ppermute | solution.py:285
  48.5 23.1 %collective-permute-start.13 = (bf16[128,1024]{1,0:T(8,128)(2,1)S(1)}, bf16[128,1024]{1,0:T(8,128)(2,1)S(1)}, u32[]{:S(2)}, u32[]{:S(2)}) collective-permute-start(bf16[128,1024]{1,0:T(8,128)(2,1)S(1)} %get-tuple-element.36), channel_id=1, source_target_pairs={{0,8},{4,12},{8,0},{12,4},{1,9},{5,13},{9,1},{13,5},{2,10},{6,14},... | collective-permute-start | bytes 786440 | tf_op jit(solution)/shard_map/ppermute | solution.py:285
  55.4 22.9 %collective-permute-start.14 = (bf16[128,1024]{1,0:T(8,128)(2,1)S(1)}, bf16[128,1024]{1,0:T(8,128)(2,1)S(1)}, u32[]{:S(2)}, u32[]{:S(2)}) collective-permute-start(bf16[128,1024]{1,0:T(8,128)(2,1)S(1)} %get-tuple-element.37), channel_id=1, source_target_pairs={{0,12},{4,8},{8,4},{12,0},{1,13},{5,9},{9,5},{13,1},{2,14},{6,10},... | collective-permute-start | bytes 786440 | tf_op jit(solution)/shard_map/ppermute | solution.py:285
  63.7 15.5 %collective-permute-start.15 = (bf16[128,1024]{1,0:T(8,128)(2,1)S(1)}, bf16[128,1024]{1,0:T(8,128)(2,1)S(1)}, u32[]{:S(2)}, u32[]{:S(2)}) collective-permute-start(bf16[128,1024]{1,0:T(8,128)(2,1)S(1)} %get-tuple-element.38.refs_0_), channel_id=1, source_target_pairs={{0,4},{4,0},{8,12},{12,8},{1,5},{5,1},{9,13},{13,9},{2,6},{6,2},{1... | collective-permute-start | bytes 786440 | tf_op jit(solution)/shard_map/ppermute | solution.py:285
  70.2 8.9 %collective-permute-start.17 = (bf16[128,1024]{1,0:T(8,128)(2,1)S(1)}, bf16[128,1024]{1,0:T(8,128)(2,1)S(1)}, u32[]{:S(2)}, u32[]{:S(2)}) collective-permute-start(bf16[128,1024]{1,0:T(8,128)(2,1)S(1)} %collective-permute-done.16.refs_1_), channel_id=1, source_target_pairs={{0,4},{4,0},{8,12},{12,8},{1,5},{5,1},{9,13},{13,9},{2,6},{6,2},{1... | collective-permute-start | bytes 786440 | tf_op jit(solution)/shard_map/ppermute | solution.py:285
  71.6 7.6 %collective-permute-start.19 = (bf16[128,1024]{1,0:T(8,128)(2,1)S(1)}, bf16[128,1024]{1,0:T(8,128)(2,1)S(1)}, u32[]{:S(2)}, u32[]{:S(2)}) collective-permute-start(bf16[128,1024]{1,0:T(8,128)(2,1)S(1)} %collective-permute-done.18.refs_2_), channel_id=1, source_target_pairs={{0,4},{4,0},{8,12},{12,8},{1,5},{5,1},{9,13},{13,9},{2,6},{6,2},{1... | collective-permute-start | bytes 786440 | tf_op jit(solution)/shard_map/ppermute | solution.py:285
  71.6 7.6 %collective-permute-start.21 = (bf16[128,1024]{1,0:T(8,128)(2,1)S(1)}, bf16[128,1024]{1,0:T(8,128)(2,1)S(1)}, u32[]{:S(2)}, u32[]{:S(2)}) collective-permute-start(bf16[128,1024]{1,0:T(8,128)(2,1)S(1)} %collective-permute-done.20.refs_3_), channel_id=1, source_target_pairs={{0,4},{4,0},{8,12},{12,8},{1,5},{5,1},{9,13},{13,9},{2,6},{6,2},{1... | collective-permute-start | bytes 786440 | tf_op jit(solution)/shard_map/ppermute | solution.py:285

commit v3 on v2

v3 whole, which is shorter than its diff:
```python
import functools
import math

import jax
import jax.numpy as jnp
from jax import lax
from jax.experimental import pallas as pl
from jax.experimental.pallas import tpu as pltpu
from jax.sharding import PartitionSpec as P


HQ = 32
KVH = 8
HD = 128
GROUP = HQ // KVH
FACTOR = 1.0 / math.sqrt(HD)
SCALE2 = FACTOR * math.log2(math.e)
MIB = 1 << 20
WARM_FLOPS = 1 << 33
EARLY = 2

NT = (((1,), (1,)), ((), ()))
NN = (((1,), (0,)), ((), ()))
BF16 = jnp.bfloat16
F32 = jnp.float32


VMEM = pl.BlockSpec(memory_space=pltpu.VMEM)
HBM = pl.BlockSpec(memory_space=pltpu.HBM)


def call(kernel, out_shape, args, flops=1 << 20, limit=20 * MIB, hbm=(), scratch=()):
    def body(*refs):
        kernel((lax.axis_index("key"), lax.axis_index("qry")), *refs)

    return pl.pallas_call(
        body,
        in_specs=[VMEM] * len(args),
        out_specs=[HBM if i in hbm else VMEM for i in range(len(out_shape))]
        if isinstance(out_shape, list)
        else VMEM,
        out_shape=out_shape,
        scratch_shapes=list(scratch),
        cost_estimate=pl.CostEstimate(flops=flops, bytes_accessed=MIB, transcendentals=0),
        compiler_params=pltpu.CompilerParams(vmem_limit_bytes=limit),
    )(*args)


def shaped(shape, dtype):
    return jax.ShapeDtypeStruct(tuple(shape), dtype)


def dot(a, b, dims):
    return lax.dot_general(a, b, dims, preferred_element_type=F32)


def stack_heads(ref, rows, base, count):
    parts = [ref[:rows, base + h * HD : base + (h + 1) * HD] for h in range(count)]
    return jnp.concatenate(parts, axis=0)


def columns_of(rows):
    n, width = rows.shape
    pad = jnp.zeros((128 - n, width), F32)
    return jnp.concatenate([rows, pad], axis=0).T


def rows_of(columns, height):
    rows = columns[0].shape[0]
    lane = lax.broadcasted_iota(jnp.int32, (rows, 128), 1)
    tile = jnp.zeros((rows, 128), F32)
    for i, c in enumerate(columns):
        tile = jnp.where(lane == i, c, tile)
    return tile.T[:height]


def kv_column(scal, p, i, ups, hp):
    g = ((scal[0] ^ p) * ups + i) * hp // GROUP
    return pl.ds(pl.multiple_of(g * HD, HD), HD)


def fwd_unit(hp, q, k, v, o_ref, e_ref, base, rows):
    s = dot(q, k, NT)
    m = jnp.max(s, axis=1, keepdims=True)
    e = jnp.exp2((s - m) * SCALE2)
    l = jnp.sum(e, axis=1, keepdims=True)
    e = e.astype(BF16)
    e_ref[base // HD * rows : (base // HD + hp) * rows] = e
    o = dot(e, v, NN).astype(BF16)
    cols = []
    for h in range(hp):
        o_ref[:, base + h * HD : base + (h + 1) * HD] = o[h * rows : (h + 1) * rows]
    for x in (m, l):
        cols += [x[h * rows : (h + 1) * rows] for h in range(hp)]
    return rows_of(cols, 2 * hp)


def fwd_kernel(hp, ups, places, scal, *refs):
    n = len(places)
    q_refs, (k_ref, v_ref) = refs[:n], refs[n : n + 2]
    o_refs, e_refs, st_ref = refs[-2 * n - 1 : -n - 1], refs[-n - 1 : -1], refs[-1]
    rows = q_refs[0].shape[0]
    for at, p in enumerate(places):
        for i in range(ups):
            col = kv_column(scal, p, i, ups, hp)
            base = i * hp * HD
            q = stack_heads(q_refs[at], rows, base, hp)
            st_ref[at * ups + i] = fwd_unit(
                hp, q, k_ref[:, col], v_ref[:, col], o_refs[at], e_refs[at], base, rows
            )


def fwd_shapes(n, rows, wide, nk, hp, ups):
    out = [shaped((rows, wide), BF16)] * n
    out += [shaped((rows * wide // HD, nk), BF16)] * n
    return out + [shaped((n * ups, 2 * hp, rows), F32)]


def warm_kernel(scal, out_ref):
    out_ref[...] = jnp.zeros_like(out_ref)


def warm_call():
    return call(warm_kernel, shaped((8, 128), F32), [], flops=WARM_FLOPS)


def fwd_call(places, q, keys, values, hp, ups, after=()):
    rows, wide = q[places[0]].shape
    nk = keys.shape[0]
    n = len(places)
    res = call(
        functools.partial(fwd_kernel, hp, ups, places),
        fwd_shapes(n, rows, wide, nk, hp, ups),
        [q[p] for p in places] + [keys, values] + list(after),
        flops=4 * n * rows * wide * nk,
    )
    return res[:n], res[n : 2 * n], res[-1]


def delta_kernel(hp, ups, places, whole, scal, *refs):
    n = len(places)
    o_refs, g_refs, out_ref = refs[:n], refs[n : 2 * n], refs[-1]
    st_refs = refs[2 * n : -1]
    u = 0
    if whole:
        u = whole - n * ups
        out_ref[:u] = st_refs[-1][...]
        st_refs = st_refs[:-1]
    stats = [(ref, i) for ref in st_refs for i in range(ref.shape[0])]
    for at in range(n):
        for i in range(ups):
            cols = []
            for h in range(hp):
                col = slice((i * hp + h) * HD, (i * hp + h + 1) * HD)
                product = o_refs[at][:, col].astype(F32) * g_refs[at][:, col].astype(F32)
                cols.append(jnp.sum(product, axis=1, keepdims=True))
            ref, m = stats[at * ups + i]
            out_ref[u, : 2 * hp] = ref[m]
            out_ref[u, 2 * hp : 3 * hp] = rows_of(cols, hp)
            u += 1


def split_bf16(x):
    parts = []
    for _ in range(3):
        parts.append(x.astype(BF16))
        x = x - parts[-1].astype(F32)
    return parts


def stats_kernel(hp, ups, n, unit_z, late, split, per_z, scal, *refs):
    st_refs, parts = refs[:n], refs[n : 3 * n]
    ld_ref, own_ref, early_ref = refs[3 * n : 3 * n + 3]
    outs = refs[3 * n + 3 :]
    for p in range(n):
        for i in range(ups):
            rows = [st_refs[q][(p ^ q) * ups + i] for q in range(n)]
            peak = rows[0][:hp]
            for x in rows[1:]:
                peak = jnp.maximum(peak, x[:hp])
            total = jnp.zeros_like(peak)
            delta = jnp.zeros_like(peak)
            for x in rows:
                w = jnp.exp2((x[:hp] - peak) * SCALE2)
                total += w * x[hp : 2 * hp]
                delta += w * x[2 * hp : 3 * hp]
            both = jnp.concatenate([peak * SCALE2 + jnp.log2(total), delta / total], axis=0)
            ld_ref[(scal[0] ^ p) * ups + i] = both
    own_ref[...] = ld_ref[pl.ds(scal[1] * unit_z, unit_z)]
    early_ref[...] = ld_ref[pl.ds((scal[1] ^ EARLY) * unit_z, unit_z)]
    for at, j in enumerate(late):
        pack_block(split, per_z, n, j, scal, parts, outs[at])
        block = ld_ref[pl.ds((scal[1] ^ j) * unit_z, unit_z)]
        flat = jnp.concatenate([block[u] for u in range(unit_z)], axis=0)
        height, rows = flat.shape
        for third, x in enumerate(split_bf16(flat)):
            outs[at][rows : rows + height, third * rows : (third + 1) * rows] = x


def out_kernel(hp, ups, n, scal, ld_ref, *refs):
    st_refs, parts, out_ref = refs[:n], refs[n : 2 * n], refs[2 * n]
    for i in range(ups):
        norm = ld_ref[scal[0] * ups + i][:hp]
        weights = [jnp.exp2(st_refs[q][q * ups + i][:hp] * SCALE2 - norm) for q in range(n)]
        cols = columns_of(jnp.concatenate(weights, axis=0))
        for h in range(hp):
            at = slice((i * hp + h) * HD, (i * hp + h + 1) * HD)
            total = None
            for q in range(n):
                lane = q * hp + h
                term = parts[q][:, at].astype(F32) * cols[:, lane : lane + 1]
                total = term if total is None else total + term
            out_ref[:, at] = total.astype(BF16)


def dq_kernel(hp, ups, places, scal, *refs):
    n = len(places)
    e_refs, g_refs = refs[:n], refs[n : 2 * n]
    k_ref, v_ref, ld_ref, st_ref = refs[2 * n : 2 * n + 4]
    dq_refs = refs[-n:]
    rows = g_refs[0].shape[0]
    for at, p in enumerate(places):
        for i in range(ups):
            col = kv_column(scal, p, i, ups, hp)
            base = i * hp * HD
            ld = ld_ref[(scal[0] ^ p) * ups + i]
            weight = jnp.exp2(st_ref[p * ups + i][:hp] * SCALE2 - ld[:hp]) * FACTOR
            cols = columns_of(jnp.concatenate([weight, ld[hp:]], axis=0))
            delta = jnp.concatenate([cols[:, hp + h : hp + h + 1] for h in range(hp)], axis=0)
            e = e_refs[at][base // HD * rows : (base // HD + hp) * rows]
            gp = dot(stack_heads(g_refs[at], rows, base, hp), v_ref[:, col], NT)
            ds = (e.astype(F32) * (gp - delta)).astype(BF16)
            dq = dot(ds, k_ref[:, col], NN)
            for h in range(hp):
                block = dq[h * rows : (h + 1) * rows] * cols[:, h : h + 1]
                dq_refs[at][:, base + h * HD : base + (h + 1) * HD] = block.astype(BF16)


def dq_call(places, e, g, keys, values, ld, own, hp, ups):
    rows, wide = g[places[0]].shape
    return call(
        functools.partial(dq_kernel, hp, ups, places),
        [shaped((rows, wide), BF16)] * len(places),
        [e[p] for p in places] + [g[p] for p in places] + [keys, values, ld, own],
        flops=4 * len(places) * rows * wide * keys.shape[0],
    )


def pack_block(split, per_z, n, j, scal, parts, out, other=None):
    rows, width = parts[0].shape[0], parts[0].shape[1] // split
    share = scal[0] % split if split > 1 else 0
    for i in range(per_z):
        place = scal[0] ^ ((scal[1] ^ j) * per_z + i)
        for p in range(n):

            @pl.when(place == p)
            def _():
                for kind in range(2):
                    col = slice((kind * per_z + i) * width, (kind * per_z + i + 1) * width)
                    for which, ref in enumerate((out, other)):
                        if ref is not None:
                            start = pl.multiple_of((share ^ which) * width, HD) if split > 1 else 0
                            ref[:rows, col] = parts[kind * n + p][:, pl.ds(start, width)]


def pack_kernel(split, per_z, n, scal, *refs):
    parts, outs = refs[: 2 * n], refs[2 * n :]
    pack_block(split, per_z, n, EARLY, scal, parts, outs[0])
    pack_block(split, per_z, n, 0, scal, parts, outs[1], outs[2] if split > 1 else None)


def dkv_kernel(hp, kvl, rows, js, halves, first_call, last_call, job, n_job, scal, *refs):
    n = len(js)
    own_ld = [j for j in js if j in (0, EARLY)]
    qg_refs, refs = refs[: n * halves], refs[n * halves :]
    ld_refs, refs = dict(zip(own_ld, refs)), refs[len(own_ld) :]
    k_ref, v_ref = refs[:2]
    priors, refs = ((None, refs[2:]) if first_call else (refs[2 : 2 + 2 * halves], refs[2 + 2 * halves :]))
    job_refs, refs = refs[:n_job], refs[n_job:]
    outs, refs = refs[: 2 if last_call else 2 * halves], refs[2 if last_call else 2 * halves :]
    pending = []
    if job is not None:
        job_out, job_scratch, job_sem = refs[0], refs[1], refs[2]
        refs = refs[3:]
        job(scal, *job_refs, job_scratch)
        copy = pltpu.make_async_copy(job_scratch, job_out, job_sem)
        copy.start()
        pending.append(copy)
    nh = kvl // halves
    sub = GROUP // hp
    for half in range(halves):
        first = ((scal[0] % 2) ^ half) * nh if halves > 1 else 0
        for g in range(nh):
            col = pl.ds(pl.multiple_of((scal[1] * kvl + first + g) * HD, HD), HD)
            here = slice(g * HD, (g + 1) * HD)
            k, v = k_ref[:, col], v_ref[:, col]
            dk = dv = None
            if priors:
                dk, dv = priors[2 * half][:, here], priors[2 * half + 1][:, here]
            for at, j in enumerate(js):
                qg = qg_refs[half * n + at]
                base = g * GROUP * HD
                qs = stack_heads(qg, rows, base, GROUP)
                gs = stack_heads(qg, rows, nh * GROUP * HD + base, GROUP)
                units = []
                for u in range(sub):
                    unit = (first + g) * sub + u
                    if j in own_ld:
                        units.append(ld_refs[j][unit])
                    else:
                        thirds = [qg[rows:, t * rows : (t + 1) * rows].astype(F32) for t in range(3)]
                        flat = thirds[0] + thirds[1] + thirds[2]
                        total = flat[: 2 * hp]
                        for m in range(1, kvl * sub):
                            total = jnp.where(unit == m, flat[m * 2 * hp : (m + 1) * 2 * hp], total)
                        units.append(total)
                norm = jnp.concatenate(
                    [units[h // hp][h % hp : h % hp + 1] for h in range(GROUP)], axis=1
                )
                delta = jnp.concatenate(
                    [units[h // hp][hp + h % hp : hp + h % hp + 1] for h in range(GROUP)], axis=1
                )
                s = dot(k, qs, NT)
                e = jnp.exp2(s * SCALE2 - norm)
                gp = dot(v, gs, NT)
                ds = (e * (gp - delta)).astype(BF16)
                dv_z = dot(e.astype(BF16), gs, NN)
                dk_z = dot(ds, qs, NN)
                dv = dv_z if dv is None else dv + dv_z
                dk = dk_z if dk is None else dk + dk_z
            if last_call:
                done, sem = refs[0], refs[1]
                mine = pl.ds(pl.multiple_of((first + g) * HD, HD), HD)
                for kind, x in enumerate((dk * FACTOR, dv)):
                    buf = done.at[half * nh + g, kind]
                    buf[...] = x.astype(BF16)
                    copy = pltpu.make_async_copy(buf, outs[kind].at[:, mine], sem.at[half * nh + g, kind])
                    copy.start()
                    pending.append(copy)
            else:
                outs[2 * half][:, here] = dk
                outs[2 * half + 1][:, here] = dv
    for copy in pending:
        copy.wait()


def dkv_call(js, qg, rows, keys, values, ld, hp, kvl, priors=(), last=False, job=None):
    halves = len(qg)
    nk = keys.shape[0]
    out = [shaped((nk, kvl * HD), BF16)] * 2
    if not last:
        out = [shaped((nk, kvl // halves * HD), F32)] * (2 * halves)
    scratch, hbm, job_args, n_out = [], (0, 1) if last else (), [], len(out)
    kernel = None
    if job is not None:
        kernel, job_args, job_shape = job
        out = out + [job_shape]
        hbm += (n_out,)
        scratch += [pltpu.VMEM(job_shape.shape, job_shape.dtype), pltpu.SemaphoreType.DMA(())]
    if last:
        scratch += [pltpu.VMEM((kvl, 2, nk, HD), BF16), pltpu.SemaphoreType.DMA((kvl, 2))]
    args = [half[j] for half in qg for j in js] + [ld[j] for j in js if j in (0, EARLY)]
    return call(
        functools.partial(
            dkv_kernel, hp, kvl, rows, js, halves, not priors, last, kernel, len(job_args)
        ),
        out,
        args + [keys, values] + list(priors) + job_args,
        flops=8 * len(js) * rows * GROUP * kvl * nk * HD,
        limit=24 * MIB,
        hbm=hbm,
        scratch=scratch,
    )


def sum_kernel(scal, *refs):
    total = refs[0][...].astype(F32)
    for r in refs[1:-1]:
        total += r[...].astype(F32)
    refs[-1][...] = total.astype(BF16)


def program(queries, keys, values, out_grad):
    n_key, n_qry = lax.axis_size("key"), lax.axis_size("qry")
    rows, wide = queries.shape
    hps = HQ // n_key
    hp = min(hps, GROUP)
    ups = hps // hp
    kvl = KVH // n_qry
    per_z = n_key // n_qry
    split = 2 if (kvl % 2 == 0 and per_z == 1) else 1
    unit_z = kvl * GROUP // hp

    def swap(x, p, axis="key"):
        if p == 0:
            return x
        return lax.ppermute(x, axis, [(i, i ^ p) for i in range(lax.axis_size(axis))])

    q, g = {0: queries}, {0: out_grad}
    bit = n_key // 2
    while bit:
        for p in list(q):
            q[p ^ bit] = swap(q[p], bit)
            g[p ^ bit] = swap(g[p], bit)
        bit //= 2

    o_part, e_part, st = {}, {}, {}
    for p in range(0, n_key, 2):
        after = [] if p else [warm_call()]
        o, e, st[p] = fwd_call((p, p + 1), q, keys, values, hp, ups, after)
        for at in range(2):
            o_part[p + at], e_part[p + at] = o[at], e[at]
    ql, gl, ol = ([x[p] for p in range(n_key)] for x in (q, g, o_part))

    width = 2 * per_z * wide // split
    block = shaped((rows, width), BF16)
    early, *own_blocks = call(
        functools.partial(pack_kernel, split, per_z, n_key), [block] * (1 + split), ql + gl
    )

    def delta_call(places, stats, whole=0):
        n = whole or len(places) * ups
        return call(
            functools.partial(delta_kernel, hp, ups, places, whole),
            shaped((n, 3 * hp, rows), F32),
            [ol[p] for p in places] + [gl[p] for p in places] + stats,
        )

    own = delta_call((0, 1), [st[0]])
    remote = [st[p] for p in range(2, n_key, 2)]
    own = delta_call(tuple(range(2, n_key)), remote + [own], n_key * ups)
    stats = [swap(own, p) for p in range(n_key)]
    o_recv = [swap(ol[p], p) for p in range(n_key)]
    late = tuple(j for j in range(1, n_qry) if j != EARLY)
    units = shaped((unit_z, 2 * hp, rows), F32)
    ld, ld_own, ld_early, *late_blocks = call(
        functools.partial(stats_kernel, hp, ups, n_key, unit_z, late, split, per_z),
        [shaped((n_key * ups, 2 * hp, rows), F32), units, units]
        + [shaped((rows + unit_z * 2 * hp, width), BF16)] * len(late),
        stats + ql + gl,
    )
    mine_z = {0: own_blocks[0], EARLY: swap(early, EARLY, "qry")}
    for j, x in zip(late, late_blocks):
        mine_z[j] = swap(x, j, "qry")
    ld_z = {0: ld_own, EARLY: swap(ld_early, EARLY, "qry")}

    dq_recv = [None] * n_key
    for p in reversed(range(0, n_key, 2)):
        dqs = dq_call((p, p + 1), e_part, g, keys, values, ld, own, hp, ups)
        for at, dq in enumerate(dqs):
            dq_recv[p + at] = swap(dq, p + at)

    blocks = [mine_z]
    if split == 2:
        blocks.append({0: own_blocks[1]})
        for j in range(1, n_qry):
            blocks[1][j] = swap(mine_z[j], 1)
    result = shaped((rows, wide), BF16)
    combine = (functools.partial(out_kernel, hp, ups, n_key), [ld] + stats + o_recv, result)
    total = (sum_kernel, dq_recv, result)

    def add(js, priors=(), last=False, job=None):
        return dkv_call(js, blocks, rows, keys, values, ld_z, hp, kvl, priors, last, job)

    acc = add((0,))
    *acc, attn_out = add((EARLY,), acc, job=combine)
    key_out, value_out, query_out = add(late, acc, last=True, job=total)
    return (attn_out, query_out, key_out, value_out)


def solution(mesh):
    in_specs = (
        P(("ckpt", "qry"), "key"),
        P(("ckpt", "key"), None),
        P(("ckpt", "key"), None),
        P(("ckpt", "qry"), "key"),
    )
    out_specs = (
        P(("ckpt", "qry"), "key"),
        P(("ckpt", "qry"), "key"),
        P(("ckpt", "key"), "qry"),
        P(("ckpt", "key"), "qry"),
    )
    return jax.shard_map(
        program, mesh=mesh, in_specs=in_specs, out_specs=out_specs, check_vma=False
    )
```

time: 85 us -> 77.5 us (0.912)
  the two profiles are of different devices: /device:TPU:15 before, /device:TPU:0 now
where the time goes in v3:
time: 77.5 us; the launch traced here: 77.1 us
  waiting for transfers between devices  32.2 us (42%)
  Pallas kernels  24.8 us (32%)
  starting transfers between devices  19.1 us (25%)
  between operations  0.98 us (1%)
    ppermute x22, waiting for transfers between devices, swap(): lax.ppermute(x, axis, [(i, i ^ p) for i in range(lax.axis_size(axis))])  32.2 us
    pallas_call x12, Pallas kernels, call(): pl.pallas_call(body, in_specs=[VMEM] * len(args), out_specs=[HBM if i in...  24.8 us
    ppermute x22, starting transfers between devices, swap(): lax.ppermute(x, axis, [(i, i ^ p) for i in range(lax.axis_size(axis))])  19.1 us
  transfers between devices with their start and end apart: 22, of which 7 were waited for; matrix products, arithmetic and copies ran while one was open for 0% of the time, Pallas kernels for 25%

profile of v3, /device:TPU:0, one launch (start us, length us, event | category | flops | bytes accessed | tf_op | source)
XLA Modules:
  0.0 77.1 jit_solution(10718638967029299414)
XLA Ops:
  0.7 3.0 %collective-permute-start.1 = (bf16[128,1024]{1,0:T(8,128)(2,1)}, bf16[128,1024]{1,0:T(8,128)(2,1)S(1)}, u32[]{:S(2)}, u32[]{:S(2)}) collective-permute-start(bf16[128,1024]{1,0:T(8,128)(2,1)} %refs_4_.8), channel_id=1, source_target_pairs={{0,8},{4,12},{8,0},{12,4},{1,9},{5,13},{9,1},{13,5},{2,10},{6,14},... | collective-permute-start | bytes 786440 | tf_op jit(solution)/shard_map/ppermute | solution.py:397
  3.7 0.1 collective-permute-start.4
  3.8 0.0 collective-permute-start
  3.8 0.5 collective-permute-start.3
  4.3 6.8 %collective-permute-done.1.refs_2_.refs_0_.refs_6_ = bf16[128,1024]{1,0:T(8,128)(2,1)S(1)} collective-permute-done((bf16[128,1024]{1,0:T(8,128)(2,1)}, bf16[128,1024]{1,0:T(8,128)(2,1)S(1)}, u32[]{:S(2)}, u32[]{:S(2)}) %collective-permute-start.1) | collective-permute-done | bytes 262176 | tf_op jit(solution)/shard_map/ppermute | solution.py:397
  11.1 4.8 %collective-permute-done.4.refs_6_.refs_2_.refs_10_ = bf16[128,1024]{1,0:T(8,128)(2,1)S(1)} collective-permute-done((bf16[128,1024]{1,0:T(8,128)(2,1)}, bf16[128,1024]{1,0:T(8,128)(2,1)S(1)}, u32[]{:S(2)}, u32[]{:S(2)}) %collective-permute-start.4) | collective-permute-done | bytes 262176 | tf_op jit(solution)/shard_map/ppermute | solution.py:397
  15.8 0.0 collective-permute-start.5
  15.9 3.5 %shard_map.78 = (bf16[128,1024]{1,0:T(8,128)(2,1)S(1)}, bf16[128,1024]{1,0:T(8,128)(2,1)S(1)}, bf16[1024,1024]{1,0:T(8,128)(2,1)S(1)}, bf16[1024,1024]{1,0:T(8,128)(2,1)S(1)}, f32[4,8,128]{2,1,0:T(8,128)S(1)}) custom-call(bf16[128,1024]{1,0:T(8,128)(2,1)S(1)} %copy-done.3, bf16[128,1024]{1,0:T(8,128)(2,1)S(1)} %collective-permute-done.refs_1_.refs_5_, ...), custom_call_target="tpu_custom_call" | custom-call | flops 1073741824 | bytes 1048576 | tf_op jit(solution)/shard_map/pallas_call | solution.py:36
  19.3 0.6 collective-permute-start.12
  19.9 0.0 collective-permute-done.3.refs_5_.refs_3_.refs_9_
  19.9 0.5 shard_map.79.refs_5_
  20.4 0.0 collective-permute-done.2.refs_3_.refs_1_.refs_7_
  20.4 0.1 shard_map.75
  20.5 2.9 %collective-permute-start.6 = (bf16[128,1024]{1,0:T(8,128)(2,1)S(1)}, bf16[128,1024]{1,0:T(8,128)(2,1)S(1)}, u32[]{:S(2)}, u32[]{:S(2)}) collective-permute-start(bf16[128,1024]{1,0:T(8,128)(2,1)S(1)} %get-tuple-element.38), channel_id=1, source_target_pairs={{0,2},{1,3},{2,0},{3,1},{4,6},{5,7},{6,4},{7,5},{8,10},{9,11},{10,... | collective-permute-start | bytes 786440 | tf_op jit(solution)/shard_map/ppermute | solution.py:397
  23.4 3.4 %shard_map.76 = (bf16[128,1024]{1,0:T(8,128)(2,1)S(1)}, bf16[128,1024]{1,0:T(8,128)(2,1)S(1)}, bf16[1024,1024]{1,0:T(8,128)(2,1)S(1)}, bf16[1024,1024]{1,0:T(8,128)(2,1)S(1)}, f32[4,8,128]{2,1,0:T(8,128)S(1)}) custom-call(bf16[128,1024]{1,0:T(8,128)(2,1)S(1)} %collective-permute-done.1.refs_2_.refs_0_.refs_6_, ...), custom_call_target="tpu_custom_call" | custom-call | flops 1073741824 | bytes 1048576 | tf_op jit(solution)/shard_map/pallas_call | solution.py:36
  26.8 0.5 shard_map.80.refs_0_.refs_10_.refs_7_
  27.3 0.9 %collective-permute-start.10 = (f32[8,12,128]{2,1,0:T(8,128)S(1)}, f32[8,12,128]{2,1,0:T(8,128)S(1)}, u32[]{:S(2)}, u32[]{:S(2)}) collective-permute-start(f32[8,12,128]{2,1,0:T(8,128)S(1)} %shard_map.80.refs_0_.refs_10_.refs_7_), channel_id=1, source_target_pairs={{0,12},{4,8},{8,4},{12,0},{1,13},{5,9},{9,5},{13,1},{2,14},{6,10},... | collective-permute-start | bytes 147464 | tf_op jit(solution)/shard_map/ppermute | solution.py:397
  28.1 0.7 collective-permute-start.8
  28.9 0.6 collective-permute-start.9
  29.5 2.2 %collective-permute-done.10.refs_3_.refs_13_ = f32[8,12,128]{2,1,0:T(8,128)S(1)} collective-permute-done((f32[8,12,128]{2,1,0:T(8,128)S(1)}, f32[8,12,128]{2,1,0:T(8,128)S(1)}, u32[]{:S(2)}, u32[]{:S(2)}) %collective-permute-start.10) | collective-permute-done | bytes 49184 | tf_op jit(solution)/shard_map/ppermute | solution.py:397
  31.7 0.0 collective-permute-done.8.refs_1_.refs_11_
  31.7 1.4 %collective-permute-done.9.refs_2_.refs_12_ = f32[8,12,128]{2,1,0:T(8,128)S(1)} collective-permute-done((f32[8,12,128]{2,1,0:T(8,128)S(1)}, f32[8,12,128]{2,1,0:T(8,128)S(1)}, u32[]{:S(2)}, u32[]{:S(2)}) %collective-permute-start.9) | collective-permute-done | bytes 49184 | tf_op jit(solution)/shard_map/ppermute | solution.py:397
  33.1 0.3 shard_map.81
  33.5 1.6 %collective-permute-start.15 = (bf16[144,1024]{1,0:T(8,128)(2,1)S(1)}, bf16[144,1024]{1,0:T(8,128)(2,1)S(1)}, u32[]{:S(2)}, u32[]{:S(2)}) collective-permute-start(bf16[144,1024]{1,0:T(8,128)(2,1)S(1)} %get-tuple-element.55), channel_id=1, source_target_pairs={{0,1},{1,0},{2,3},{3,2},{4,5},{5,4},{6,7},{7,6},{8,9},{9,8},{10,11... | collective-permute-start | bytes 884744 | tf_op jit(solution)/shard_map/ppermute | solution.py:397
  35.1 0.2 collective-permute-start.16
  35.3 1.7 %collective-permute-start.11 = (f32[2,8,128]{2,1,0:T(8,128)S(1)}, f32[2,8,128]{2,1,0:T(8,128)S(1)}, u32[]{:S(2)}, u32[]{:S(2)}) collective-permute-start(f32[2,8,128]{2,1,0:T(8,128)S(1)} %get-tuple-element.45), channel_id=1, source_target_pairs={{0,2},{1,3},{2,0},{3,1},{4,6},{5,7},{6,4},{7,5},{8,10},{9,11},{10,... | collective-permute-start | bytes 24584 | tf_op jit(solution)/shard_map/ppermute | solution.py:397
  37.0 0.0 collective-permute-done.12.refs_15_
  37.0 1.3 %collective-permute-start.13 = (bf16[128,1024]{1,0:T(8,128)(2,1)S(1)}, bf16[128,1024]{1,0:T(8,128)(2,1)S(1)}, u32[]{:S(2)}, u32[]{:S(2)}) collective-permute-start(bf16[128,1024]{1,0:T(8,128)(2,1)S(1)} %get-tuple-element.39.refs_0_), channel_id=1, source_target_pairs={{0,8},{4,12},{8,0},{12,4},{1,9},{5,13},{9,1},{13,5},{2,10},{6,14},... | collective-permute-start | bytes 786440 | tf_op jit(solution)/shard_map/ppermute | solution.py:397
  38.3 11.3 %collective-permute-done.11.refs_2_ = f32[2,8,128]{2,1,0:T(8,128)S(1)} collective-permute-done((f32[2,8,128]{2,1,0:T(8,128)S(1)}, f32[2,8,128]{2,1,0:T(8,128)S(1)}, u32[]{:S(2)}, u32[]{:S(2)}) %collective-permute-start.11) | collective-permute-done | bytes 8224 | tf_op jit(solution)/shard_map/ppermute | solution.py:397
  49.7 0.4 collective-permute-start.14
  50.1 0.0 collective-permute-done.6.refs_0_
  50.1 1.8 %collective-permute-start.7 = (bf16[128,1024]{1,0:T(8,128)(2,1)S(1)}, bf16[128,1024]{1,0:T(8,128)(2,1)S(1)}, u32[]{:S(2)}, u32[]{:S(2)}) collective-permute-start(bf16[128,1024]{1,0:T(8,128)(2,1)S(1)} %collective-permute-done.6.refs_0_), channel_id=1, source_target_pairs={{0,4},{4,0},{8,12},{12,8},{1,5},{5,1},{9,13},{13,9},{2,6},{6,2},{1... | collective-permute-start | bytes 786440 | tf_op jit(solution)/shard_map/ppermute | solution.py:397
  51.9 2.8 %shard_map.85 = (bf16[128,1024]{1,0:T(8,128)(2,1)S(1)}, bf16[128,1024]{1,0:T(8,128)(2,1)S(1)}) custom-call(bf16[1024,1024]{1,0:T(8,128)(2,1)S(1)} %get-tuple-element.65.refs_0_, bf16[1024,1024]{1,0:T(8,128)(2,1)S(1)} %get-tuple-element.66.refs_1_, bf16[128,1024]{1,0:T(8,128)(2,1)S(1)} %collective-permute-done.4.refs_6_.refs_2_.refs_10_, ...), custom_call_target="tpu_custom_call" | custom-call | flops 1073741824 | bytes 1048576 | tf_op jit(solution)/shard_map/pallas_call | solution.py:36
  54.7 0.1 collective-permute-start.17
  54.8 0.0 collective-permute-done.16.refs_1_
  54.8 0.5 collective-permute-start.18
  55.3 2.7 %shard_map.84 = (bf16[128,1024]{1,0:T(8,128)(2,1)S(1)}, bf16[128,1024]{1,0:T(8,128)(2,1)S(1)}) custom-call(bf16[1024,1024]{1,0:T(8,128)(2,1)S(1)} %get-tuple-element.61.refs_0_, bf16[1024,1024]{1,0:T(8,128)(2,1)S(1)} %get-tuple-element.62.refs_1_, bf16[128,1024]{1,0:T(8,128)(2,1)S(1)} %copy-done.2, ...), custom_call_target="tpu_custom_call" | custom-call | flops 1073741824 | bytes 1048576 | tf_op jit(solution)/shard_map/pallas_call | solution.py:36
  58.0 0.1 collective-permute-start.20
  58.1 0.0 collective-permute-done.14.refs_17_
  58.1 1.4 %collective-permute-start.21 = (bf16[128,1024]{1,0:T(8,128)(2,1)S(1)}, bf16[128,1024]{1,0:T(8,128)(2,1)S(1)}, u32[]{:S(2)}, u32[]{:S(2)}) collective-permute-start(bf16[128,1024]{1,0:T(8,128)(2,1)S(1)} %get-tuple-element.68), channel_id=1, source_target_pairs={{0,12},{4,8},{8,4},{12,0},{1,13},{5,9},{9,5},{13,1},{2,14},{6,10},... | collective-permute-start | bytes 786440 | tf_op jit(solution)/shard_map/ppermute | solution.py:397
  59.5 0.7 collective-permute-start.19
  60.2 2.4 %shard_map.82 = (f32[1024,128]{1,0:T(8,128)S(1)}, f32[1024,128]{1,0:T(8,128)S(1)}, f32[1024,128]{1,0:T(8,128)S(1)}, f32[1024,128]{1,0:T(8,128)S(1)}) custom-call(bf16[128,1024]{1,0:T(8,128)(2,1)S(1)} %get-tuple-element.46.refs_0_, bf16[128,1024]{1,0:T(8,128)(2,1)S(1)} %get-tuple-element.47.refs_1_, f32[2,8,128]{2,1,0:T(8,128)S(1)} %get-tuple-element.48.refs_2_, ...), custom_call_target="tpu_custom_call" | custom-call | flops 1073741824 | bytes 1048576 | tf_op jit(solution)/shard_map/pallas_call | solution.py:36
  62.6 2.9 %shard_map.83 = (f32[1024,128]{1,0:T(8,128)S(1)}, f32[1024,128]{1,0:T(8,128)S(1)}, f32[1024,128]{1,0:T(8,128)S(1)}, f32[1024,128]{1,0:T(8,128)S(1)}, bf16[128,1024]{1,0:T(8,128)(2,1)}) custom-call(bf16[128,1024]{1,0:T(8,128)(2,1)S(1)} %collective-permute-done.6.refs_0_, bf16[128,1024]{1,0:T(8,128)(2,1)S(1)} %collective-permute-done.7.refs_1_, ...), custom_call_target="tpu_custom_call" | custom-call | flops 1073741824 | bytes 1048576 | tf_op jit(solution)/shard_map/pallas_call | solution.py:36
  65.5 1.8 %collective-permute-done.20.refs_12_ = bf16[128,1024]{1,0:T(8,128)(2,1)S(1)} collective-permute-done((bf16[128,1024]{1,0:T(8,128)(2,1)S(1)}, bf16[128,1024]{1,0:T(8,128)(2,1)S(1)}, u32[]{:S(2)}, u32[]{:S(2)}) %collective-permute-start.20) | collective-permute-done | bytes 262176 | tf_op jit(solution)/shard_map/ppermute | solution.py:397
  67.3 3.9 %collective-permute-done.21.refs_13_ = bf16[128,1024]{1,0:T(8,128)(2,1)S(1)} collective-permute-done((bf16[128,1024]{1,0:T(8,128)(2,1)S(1)}, bf16[128,1024]{1,0:T(8,128)(2,1)S(1)}, u32[]{:S(2)}, u32[]{:S(2)}) %collective-permute-start.21) | collective-permute-done | bytes 262176 | tf_op jit(solution)/shard_map/ppermute | solution.py:397
  71.1 0.0 collective-permute-done.19.refs_11_
  71.1 0.0 collective-permute-done.17.refs_2_
  71.1 5.8 %shard_map.86 = (bf16[1024,256]{1,0:T(8,128)(2,1)}, bf16[1024,256]{1,0:T(8,128)(2,1)}, bf16[128,1024]{1,0:T(8,128)(2,1)}) custom-call(bf16[144,1024]{1,0:T(8,128)(2,1)S(1)} %collective-permute-done.15.refs_0_, bf16[144,1024]{1,0:T(8,128)(2,1)S(1)} %collective-permute-done.16.refs_1_, bf16[144,1024]{1,0:T(8,128)(2,1)S(1)} %collective-permute-done.17.refs_2_, ...), custom_call_target="tpu_custom_call" | custom-call | flops 2147483648 | bytes 1048576 | tf_op jit(solution)/shard_map/pallas_call | solution.py:36
  (16 shorter events, 0.0 us)
Async XLA Ops:
  0.6 15.2 %copy-start.3 = (bf16[128,1024]{1,0:T(8,128)(2,1)S(1)}, bf16[128,1024]{1,0:T(8,128)(2,1)}, u32[]{:S(2)}) copy-start(bf16[128,1024]{1,0:T(8,128)(2,1)} %refs_4_.8) | copy-start | bytes 786436
  0.6 15.2 %copy-start = (bf16[1024,1024]{1,0:T(8,128)(2,1)S(1)}, bf16[1024,1024]{1,0:T(8,128)(2,1)}, u32[]{:S(2)}) copy-start(bf16[1024,1024]{1,0:T(8,128)(2,1)} %refs_4_.13) | copy-start | bytes 6291460
  0.7 15.2 %copy-start.1 = (bf16[1024,1024]{1,0:T(8,128)(2,1)S(1)}, bf16[1024,1024]{1,0:T(8,128)(2,1)}, u32[]{:S(2)}) copy-start(bf16[1024,1024]{1,0:T(8,128)(2,1)} %refs_5_.5) | copy-start | bytes 6291460
  0.7 10.4 %collective-permute-start.1 = (bf16[128,1024]{1,0:T(8,128)(2,1)}, bf16[128,1024]{1,0:T(8,128)(2,1)S(1)}, u32[]{:S(2)}, u32[]{:S(2)}) collective-permute-start(bf16[128,1024]{1,0:T(8,128)(2,1)} %refs_4_.8), channel_id=1, source_target_pairs={{0,8},{4,12},{8,0},{12,4},{1,9},{5,13},{9,1},{13,5},{2,10},{6,14},... | collective-permute-start | bytes 786440 | tf_op jit(solution)/shard_map/ppermute | solution.py:397
  3.7 12.1 %collective-permute-start.4 = (bf16[128,1024]{1,0:T(8,128)(2,1)}, bf16[128,1024]{1,0:T(8,128)(2,1)S(1)}, u32[]{:S(2)}, u32[]{:S(2)}) collective-permute-start(bf16[128,1024]{1,0:T(8,128)(2,1)} %refs_2_.7), channel_id=1, source_target_pairs={{0,8},{4,12},{8,0},{12,4},{1,9},{5,13},{9,1},{13,5},{2,10},{6,14},... | collective-permute-start | bytes 786440 | tf_op jit(solution)/shard_map/ppermute | solution.py:397
  3.8 12.1 %collective-permute-start = (bf16[128,1024]{1,0:T(8,128)(2,1)}, bf16[128,1024]{1,0:T(8,128)(2,1)S(1)}, u32[]{:S(2)}, u32[]{:S(2)}) collective-permute-start(bf16[128,1024]{1,0:T(8,128)(2,1)} %refs_4_.8), channel_id=1, source_target_pairs={{0,4},{4,0},{8,12},{12,8},{1,5},{5,1},{9,13},{13,9},{2,6},{6,2},{1... | collective-permute-start | bytes 786440 | tf_op jit(solution)/shard_map/ppermute | solution.py:397
  3.8 16.2 %collective-permute-start.3 = (bf16[128,1024]{1,0:T(8,128)(2,1)}, bf16[128,1024]{1,0:T(8,128)(2,1)S(1)}, u32[]{:S(2)}, u32[]{:S(2)}) collective-permute-start(bf16[128,1024]{1,0:T(8,128)(2,1)} %refs_2_.7), channel_id=1, source_target_pairs={{0,4},{4,0},{8,12},{12,8},{1,5},{5,1},{9,13},{13,9},{2,6},{6,2},{1... | collective-permute-start | bytes 786440 | tf_op jit(solution)/shard_map/ppermute | solution.py:397
  11.1 9.3 %collective-permute-start.2 = (bf16[128,1024]{1,0:T(8,128)(2,1)S(1)}, bf16[128,1024]{1,0:T(8,128)(2,1)S(1)}, u32[]{:S(2)}, u32[]{:S(2)}) collective-permute-start(bf16[128,1024]{1,0:T(8,128)(2,1)S(1)} %collective-permute-done.1.refs_2_.refs_0_.refs_6_), channel_id=1, source_target_pairs={{0,4},{4,0},{8,12},{12,8},{1,5},{5,1},{9,13},{13,9},{2,6},{6,2},{1... | collective-permute-start | bytes 786440 | tf_op jit(solution)/shard_map/ppermute | solution.py:397
  15.8 4.6 %collective-permute-start.5 = (bf16[128,1024]{1,0:T(8,128)(2,1)S(1)}, bf16[128,1024]{1,0:T(8,128)(2,1)S(1)}, u32[]{:S(2)}, u32[]{:S(2)}) collective-permute-start(bf16[128,1024]{1,0:T(8,128)(2,1)S(1)} %collective-permute-done.4.refs_6_.refs_2_.refs_10_), channel_id=1, source_target_pairs={{0,4},{4,0},{8,12},{12,8},{1,5},{5,1},{9,13},{13,9},{2,6},{6,2},{1... | collective-permute-start | bytes 786440 | tf_op jit(solution)/shard_map/ppermute | solution.py:397
  15.8 4.1 %copy-start.2 = (bf16[128,1024]{1,0:T(8,128)(2,1)S(1)}, bf16[128,1024]{1,0:T(8,128)(2,1)}, u32[]{:S(2)}) copy-start(bf16[128,1024]{1,0:T(8,128)(2,1)} %refs_2_.7) | copy-start | bytes 786436
  19.3 17.7 %collective-permute-start.12 = (bf16[128,1024]{1,0:T(8,128)(2,1)S(1)}, bf16[128,1024]{1,0:T(8,128)(2,1)S(1)}, u32[]{:S(2)}, u32[]{:S(2)}) collective-permute-start(bf16[128,1024]{1,0:T(8,128)(2,1)S(1)} %get-tuple-element.43.refs_1_), channel_id=1, source_target_pairs={{0,4},{4,0},{8,12},{12,8},{1,5},{5,1},{9,13},{13,9},{2,6},{6,2},{1... | collective-permute-start | bytes 786440 | tf_op jit(solution)/shard_map/ppermute | solution.py:397
  20.5 29.6 %collective-permute-start.6 = (bf16[128,1024]{1,0:T(8,128)(2,1)S(1)}, bf16[128,1024]{1,0:T(8,128)(2,1)S(1)}, u32[]{:S(2)}, u32[]{:S(2)}) collective-permute-start(bf16[128,1024]{1,0:T(8,128)(2,1)S(1)} %get-tuple-element.38), channel_id=1, source_target_pairs={{0,2},{1,3},{2,0},{3,1},{4,6},{5,7},{6,4},{7,5},{8,10},{9,11},{10,... | collective-permute-start | bytes 786440 | tf_op jit(solution)/shard_map/ppermute | solution.py:397
  27.3 4.4 %collective-permute-start.10 = (f32[8,12,128]{2,1,0:T(8,128)S(1)}, f32[8,12,128]{2,1,0:T(8,128)S(1)}, u32[]{:S(2)}, u32[]{:S(2)}) collective-permute-start(f32[8,12,128]{2,1,0:T(8,128)S(1)} %shard_map.80.refs_0_.refs_10_.refs_7_), channel_id=1, source_target_pairs={{0,12},{4,8},{8,4},{12,0},{1,13},{5,9},{9,5},{13,1},{2,14},{6,10},... | collective-permute-start | bytes 147464 | tf_op jit(solution)/shard_map/ppermute | solution.py:397
  28.1 3.6 %collective-permute-start.8 = (f32[8,12,128]{2,1,0:T(8,128)S(1)}, f32[8,12,128]{2,1,0:T(8,128)S(1)}, u32[]{:S(2)}, u32[]{:S(2)}) collective-permute-start(f32[8,12,128]{2,1,0:T(8,128)S(1)} %shard_map.80.refs_0_.refs_10_.refs_7_), channel_id=1, source_target_pairs={{0,4},{4,0},{8,12},{12,8},{1,5},{5,1},{9,13},{13,9},{2,6},{6,2},{1... | collective-permute-start | bytes 147464 | tf_op jit(solution)/shard_map/ppermute | solution.py:397
  28.9 4.3 %collective-permute-start.9 = (f32[8,12,128]{2,1,0:T(8,128)S(1)}, f32[8,12,128]{2,1,0:T(8,128)S(1)}, u32[]{:S(2)}, u32[]{:S(2)}) collective-permute-start(f32[8,12,128]{2,1,0:T(8,128)S(1)} %shard_map.80.refs_0_.refs_10_.refs_7_), channel_id=1, source_target_pairs={{0,8},{4,12},{8,0},{12,4},{1,9},{5,13},{9,1},{13,5},{2,10},{6,14},... | collective-permute-start | bytes 147464 | tf_op jit(solution)/shard_map/ppermute | solution.py:397
  33.5 21.2 %collective-permute-start.15 = (bf16[144,1024]{1,0:T(8,128)(2,1)S(1)}, bf16[144,1024]{1,0:T(8,128)(2,1)S(1)}, u32[]{:S(2)}, u32[]{:S(2)}) collective-permute-start(bf16[144,1024]{1,0:T(8,128)(2,1)S(1)} %get-tuple-element.55), channel_id=1, source_target_pairs={{0,1},{1,0},{2,3},{3,2},{4,5},{5,4},{6,7},{7,6},{8,9},{9,8},{10,11... | collective-permute-start | bytes 884744 | tf_op jit(solution)/shard_map/ppermute | solution.py:397
  35.1 19.7 %collective-permute-start.16 = (bf16[144,1024]{1,0:T(8,128)(2,1)S(1)}, bf16[144,1024]{1,0:T(8,128)(2,1)S(1)}, u32[]{:S(2)}, u32[]{:S(2)}) collective-permute-start(bf16[144,1024]{1,0:T(8,128)(2,1)S(1)} %get-tuple-element.56), channel_id=1, source_target_pairs={{0,3},{1,2},{2,1},{3,0},{4,7},{5,6},{6,5},{7,4},{8,11},{9,10},{10,... | collective-permute-start | bytes 884744 | tf_op jit(solution)/shard_map/ppermute | solution.py:397
  35.3 14.4 %collective-permute-start.11 = (f32[2,8,128]{2,1,0:T(8,128)S(1)}, f32[2,8,128]{2,1,0:T(8,128)S(1)}, u32[]{:S(2)}, u32[]{:S(2)}) collective-permute-start(f32[2,8,128]{2,1,0:T(8,128)S(1)} %get-tuple-element.45), channel_id=1, source_target_pairs={{0,2},{1,3},{2,0},{3,1},{4,6},{5,7},{6,4},{7,5},{8,10},{9,11},{10,... | collective-permute-start | bytes 24584 | tf_op jit(solution)/shard_map/ppermute | solution.py:397
  37.0 21.0 %collective-permute-start.13 = (bf16[128,1024]{1,0:T(8,128)(2,1)S(1)}, bf16[128,1024]{1,0:T(8,128)(2,1)S(1)}, u32[]{:S(2)}, u32[]{:S(2)}) collective-permute-start(bf16[128,1024]{1,0:T(8,128)(2,1)S(1)} %get-tuple-element.39.refs_0_), channel_id=1, source_target_pairs={{0,8},{4,12},{8,0},{12,4},{1,9},{5,13},{9,1},{13,5},{2,10},{6,14},... | collective-permute-start | bytes 786440 | tf_op jit(solution)/shard_map/ppermute | solution.py:397
  49.7 8.4 %collective-permute-start.14 = (bf16[128,1024]{1,0:T(8,128)(2,1)S(1)}, bf16[128,1024]{1,0:T(8,128)(2,1)S(1)}, u32[]{:S(2)}, u32[]{:S(2)}) collective-permute-start(bf16[128,1024]{1,0:T(8,128)(2,1)S(1)} %get-tuple-element.40.refs_1_), channel_id=1, source_target_pairs={{0,12},{4,8},{8,4},{12,0},{1,13},{5,9},{9,5},{13,1},{2,14},{6,10},... | collective-permute-start | bytes 786440 | tf_op jit(solution)/shard_map/ppermute | solution.py:397
  50.1 9.4 %collective-permute-start.7 = (bf16[128,1024]{1,0:T(8,128)(2,1)S(1)}, bf16[128,1024]{1,0:T(8,128)(2,1)S(1)}, u32[]{:S(2)}, u32[]{:S(2)}) collective-permute-start(bf16[128,1024]{1,0:T(8,128)(2,1)S(1)} %collective-permute-done.6.refs_0_), channel_id=1, source_target_pairs={{0,4},{4,0},{8,12},{12,8},{1,5},{5,1},{9,13},{13,9},{2,6},{6,2},{1... | collective-permute-start | bytes 786440 | tf_op jit(solution)/shard_map/ppermute | solution.py:397
  54.7 16.4 %collective-permute-start.17 = (bf16[144,1024]{1,0:T(8,128)(2,1)S(1)}, bf16[144,1024]{1,0:T(8,128)(2,1)S(1)}, u32[]{:S(2)}, u32[]{:S(2)}) collective-permute-start(bf16[144,1024]{1,0:T(8,128)(2,1)S(1)} %collective-permute-done.15.refs_0_), channel_id=1, source_target_pairs={{0,4},{4,0},{8,12},{12,8},{1,5},{5,1},{9,13},{13,9},{2,6},{6,2},{1... | collective-permute-start | bytes 884744 | tf_op jit(solution)/shard_map/ppermute | solution.py:397
  54.8 16.4 %collective-permute-start.18 = (bf16[144,1024]{1,0:T(8,128)(2,1)S(1)}, bf16[144,1024]{1,0:T(8,128)(2,1)S(1)}, u32[]{:S(2)}, u32[]{:S(2)}) collective-permute-start(bf16[144,1024]{1,0:T(8,128)(2,1)S(1)} %collective-permute-done.16.refs_1_), channel_id=1, source_target_pairs={{0,4},{4,0},{8,12},{12,8},{1,5},{5,1},{9,13},{13,9},{2,6},{6,2},{1... | collective-permute-start | bytes 884744 | tf_op jit(solution)/shard_map/ppermute | solution.py:397
  58.0 9.2 %collective-permute-start.20 = (bf16[128,1024]{1,0:T(8,128)(2,1)S(1)}, bf16[128,1024]{1,0:T(8,128)(2,1)S(1)}, u32[]{:S(2)}, u32[]{:S(2)}) collective-permute-start(bf16[128,1024]{1,0:T(8,128)(2,1)S(1)} %get-tuple-element.67), channel_id=1, source_target_pairs={{0,8},{4,12},{8,0},{12,4},{1,9},{5,13},{9,1},{13,5},{2,10},{6,14},... | collective-permute-start | bytes 786440 | tf_op jit(solution)/shard_map/ppermute | solution.py:397
  58.1 13.0 %collective-permute-start.21 = (bf16[128,1024]{1,0:T(8,128)(2,1)S(1)}, bf16[128,1024]{1,0:T(8,128)(2,1)S(1)}, u32[]{:S(2)}, u32[]{:S(2)}) collective-permute-start(bf16[128,1024]{1,0:T(8,128)(2,1)S(1)} %get-tuple-element.68), channel_id=1, source_target_pairs={{0,12},{4,8},{8,4},{12,0},{1,13},{5,9},{9,5},{13,1},{2,14},{6,10},... | collective-permute-start | bytes 786440 | tf_op jit(solution)/shard_map/ppermute | solution.py:397
  59.5 11.6 %collective-permute-start.19 = (bf16[128,1024]{1,0:T(8,128)(2,1)S(1)}, bf16[128,1024]{1,0:T(8,128)(2,1)S(1)}, u32[]{:S(2)}, u32[]{:S(2)}) collective-permute-start(bf16[128,1024]{1,0:T(8,128)(2,1)S(1)} %get-tuple-element.64), channel_id=1, source_target_pairs={{0,4},{4,0},{8,12},{12,8},{1,5},{5,1},{9,13},{13,9},{2,6},{6,2},{1... | collective-permute-start | bytes 786440 | tf_op jit(solution)/shard_map/ppermute | solution.py:397
